TPU v7x, 32 devices: a whole 2x2x4 slice. The times are simulated.
32 devices in a mesh: row: 4 (over z), col: 8 (over y, x, core).
Axes of the slice: x: 2, y: 2, z: 4, core: 2. Of those that a mesh axis runs over, the one named last changes fastest.
Arguments:
- clean: float32 [1344, 8192], P('row', 'col'), may hold values from -6 to 6
- noise: float32 [1344, 8192], P('row', 'col'), may hold values from -6 to 6
- bucket: int32 [32], replicated, may hold values from 0 to 31
- mod_table: float32 [1, 32, 1344], replicated, may hold values from -3 to 3
- w_first: float32 [1, 1344, 1344], P(None, 'row', 'col'), may hold values from -0.15625 to 0.15625
- w_second: float32 [1, 1344, 1344], P(None, 'col', 'row'), may hold values from -0.15625 to 0.15625
Outputs:
- grad_first: float32 [1, 1344, 1344], P(None, 'row', 'col')
- grad_second: float32 [1, 1344, 1344], P(None, 'col', 'row')
All inputs are finite; a program needn't handle non-finite values.
Results may differ from a plain program's by a relative error of at most 0.018.
Values may be sent and summed in bfloat16 or wider, within the bound.
A program may use at most 64 MiB of HBM per device.

v0:
```python
import math

import jax
import jax.numpy as jnp
from jax import lax
from jax.experimental import pallas as pl
from jax.experimental.pallas import tpu as pltpu
from jax.sharding import PartitionSpec as P

PIX = 256
BUCKETS = 32


MIX_WEIGHT = 0.3
KEEP_COEF = (1.0 - MIX_WEIGHT) / math.sqrt((1.0 - MIX_WEIGHT) ** 2 + MIX_WEIGHT**2)
ADD_COEF = MIX_WEIGHT / math.sqrt((1.0 - MIX_WEIGHT) ** 2 + MIX_WEIGHT**2)
SILU_GAIN = 1.0 / 0.596
CONTRACT_LEAD = (((0,), (0,)), ((), ()))
CONTRACT_TAIL = (((1,), (1,)), ((), ()))


def noise_levels(bucket):
    return jnp.exp(-3.0 + 5.0 * (bucket.astype(jnp.float32) + 0.5) / BUCKETS)


def silu_slope(values):
    sig = jax.nn.sigmoid(values)
    return sig * (1.0 + values * (1.0 - sig))


def bucket_gains(table, picked):
    onehot = (picked[:, None] == jnp.arange(table.shape[0], dtype=jnp.int32)[None, :]).astype(
        jnp.float32
    )
    return jnp.dot(
        onehot, table, precision=lax.Precision.HIGHEST, preferred_element_type=jnp.float32
    )


def local(clean, noise, bucket, mod_table, w_first, w_second):
    rows_size = lax.axis_size("row")
    row_at = lax.axis_index("row")
    col_at = lax.axis_index("col")
    samples = bucket.shape[0]
    own_rows = clean.shape[1]
    weight_first = w_first[0]
    weight_second = w_second[0]
    table = 1.0 + mod_table[0]
    col_first = jnp.sqrt(lax.psum(jnp.sum(weight_first * weight_first, axis=0), "row") + 1.0)
    col_second = jnp.sqrt(lax.psum(jnp.sum(weight_second * weight_second, axis=0), "col") + 1.0)
    normed_first = (weight_first / col_first[None, :]).astype(jnp.bfloat16)
    normed_second = (weight_second / col_second[None, :]).astype(jnp.bfloat16)
    chan_clean, chan_noise = (
        lax.all_to_all(
            clean.astype(jnp.bfloat16), "row", split_axis=1, concat_axis=0, tiled=True
        ).astype(clean.dtype),
        lax.all_to_all(
            noise.astype(jnp.bfloat16), "row", split_axis=1, concat_axis=0, tiled=True
        ).astype(noise.dtype),
    )
    local_clean = chan_clean.T
    local_noise = chan_noise.T
    sub_rows = own_rows // rows_size
    first_row = col_at * own_rows + row_at * sub_rows
    row_sample = (first_row + jnp.arange(sub_rows, dtype=jnp.int32)) // PIX
    row_bucket = jnp.take(bucket, row_sample)
    levels = noise_levels(row_bucket)[:, None]
    spread_root = jnp.sqrt(levels * levels + 0.25)
    state_own = ((local_clean + levels * local_noise) / spread_root).astype(jnp.bfloat16)
    target = local_clean * (2.0 * levels / spread_root) - local_noise * (0.5 / spread_root)
    gains = bucket_gains(table, row_bucket)
    part_first, part_second = (
        lax.all_gather(normed_first, "col", axis=1, tiled=True),
        lax.all_gather(normed_second, "col", axis=0, tiled=True),
    )
    full_first, full_second = (
        lax.all_gather(part_first, "row", axis=0, tiled=True),
        lax.all_gather(part_second, "row", axis=1, tiled=True),
    )
    pre_act = jnp.dot(state_own, full_first, preferred_element_type=jnp.float32)
    hidden = (jax.nn.silu(pre_act) * SILU_GAIN * gains).astype(jnp.bfloat16)
    branch = jnp.dot(hidden, full_second, preferred_element_type=jnp.float32)
    state_new = (KEEP_COEF * state_own.astype(jnp.float32) + ADD_COEF * branch).astype(jnp.bfloat16)
    grad_own = (state_new.astype(jnp.float32) - target) / samples
    dbranch = (ADD_COEF * grad_own).astype(jnp.bfloat16)
    gsecond_full = lax.dot_general(
        hidden, dbranch, CONTRACT_LEAD, preferred_element_type=jnp.float32
    )
    dhidden = lax.dot_general(
        dbranch, full_second, CONTRACT_TAIL, preferred_element_type=jnp.float32
    )
    dpre = (dhidden * gains * silu_slope(pre_act) * SILU_GAIN).astype(jnp.bfloat16)
    gfirst_full = lax.dot_general(
        state_own, dpre, CONTRACT_LEAD, preferred_element_type=jnp.float32
    )
    part_gfirst, part_gsecond = (
        lax.psum_scatter(
            gfirst_full.astype(jnp.bfloat16), "col", scatter_dimension=1, tiled=True
        ).astype(jnp.float32),
        lax.psum_scatter(
            gsecond_full.astype(jnp.bfloat16), "col", scatter_dimension=0, tiled=True
        ).astype(jnp.float32),
    )
    gfirst, gsecond = (
        lax.psum_scatter(
            part_gfirst.astype(jnp.bfloat16), "row", scatter_dimension=0, tiled=True
        ).astype(jnp.float32),
        lax.psum_scatter(
            part_gsecond.astype(jnp.bfloat16), "row", scatter_dimension=1, tiled=True
        ).astype(jnp.float32),
    )
    dot_first = lax.psum(jnp.sum(weight_first * gfirst, axis=0), "row")
    dot_second = lax.psum(jnp.sum(weight_second * gsecond, axis=0), "col")
    grad_first = gfirst / col_first[None, :] - weight_first * (dot_first / col_first**3)[None, :]
    grad_second = (
        gsecond / col_second[None, :] - weight_second * (dot_second / col_second**3)[None, :]
    )
    return (grad_first[None], grad_second[None])


CORES = 2
SIDE = 2
MESH = pl.DeviceIdType.MESH
(S_UP, S_DN, S_X, S_Y, S_D0, S_D1, S_S, S_T, S_F, R_Z, R_X, R_Y, R_D0, R_D1, R_S, R_T, R_F,
 S_A0, S_A1, R_A0, R_A1, S_BX, S_CX, S_BY, S_CY, R_BX, R_CX, R_BY, R_CY, S_P, R_P, MISC) = range(32)


def round_up(size, unit):
    return -(-size // unit) * unit


def step_kernel(
    hb, ib, samples, wown, sto, gsel, w1f, w2f, out1, out2,
    w, st, tg, pre, hid, brp, brk, brr, dbr, db2, dpre, s2, d2, g,
    ra, sa, rx, ry, pz, rz, colf, sems,
):
    rows = st.shape[1] // wown.shape[2]
    hp, ip = wown.shape[1], wown.shape[2]
    chips = w.shape[1] // hp
    sub = st.shape[2]
    z = lax.axis_index("row")
    col = lax.axis_index("col")
    core = lax.rem(col, CORES)
    xy = col // CORES
    x, y = lax.rem(xy, SIDE), xy // SIDE
    xn = y * SIDE + (1 - x)
    yn = (1 - y) * SIDE + x
    dn = (1 - y) * SIDE + (1 - x)
    dev_x = (z, xn * CORES + core)
    dev_y = (z, yn * CORES + core)
    dev_p = (z, xy * CORES + 1 - core)
    up, down = (z + 1, col), (z - 1, col)
    ring = [lax.rem(z + k, rows) for k in range(rows)]

    barrier = pltpu.get_barrier_semaphore()
    peers = [dev_x, dev_y, dev_p] + [(ring[k], col) for k in range(1, rows)]
    for peer in peers:
        pl.semaphore_signal(barrier, inc=1, device_id=peer, device_id_type=MESH)

    pending = []

    def remote(src, dst, send, recv, dev):
        return pltpu.make_async_remote_copy(
            src_ref=src, dst_ref=dst, send_sem=sems.at[send[0], send[1]],
            recv_sem=sems.at[recv[0], recv[1]], device_id=dev, device_id_type=MESH,
        )

    def when(cond, fn):
        if cond is None:
            fn()
        else:
            pl.when(cond)(fn)

    def send(cond, *spec):
        when(cond, lambda: remote(*spec).start())
        pending.append((cond, spec))

    def arrive(cond, dst, recv):
        when(cond, lambda: remote(dst, dst, recv, recv, dev_p).wait_recv())

    def both(a, b):
        return b if a is None else (a if b is None else jnp.logical_and(a, b))

    def blk(zb, xyb, half=None):
        at = (pl.ds(pl.multiple_of(xyb * hp, 16), hp), pl.ds(pl.multiple_of(zb * ip, 128), ip))
        return w.at[(slice(None),) + at] if half is None else w.at[(half,) + at]

    def chan(zb):
        return pl.ds(pl.multiple_of(zb * ip, 128), ib)

    def pix(zb):
        return pl.ds(pl.multiple_of(zb * sub, 128), sub)

    local_w = pltpu.make_async_copy(wown, blk(z, xy), sems.at[MISC, 0])
    local_w.start()
    local_s = pltpu.make_async_copy(sto.at[0, :, pix(z)], st.at[core, chan(z)], sems.at[MISC, 1])
    local_s.start()
    local_t = pltpu.make_async_copy(sto.at[1, :, pix(z)], tg.at[chan(z)], sems.at[MISC, 2])
    local_t.start()
    for zb in range(rows):
        pad = slice(zb * ip + ib, (zb + 1) * ip)
        zero = jnp.zeros((ip - ib, sub), jnp.bfloat16)
        st[0, pad, :] = zero
        st[1, pad, :] = zero
        tg[pad, :] = zero
    pl.semaphore_wait(barrier, len(peers))

    def spread(cond, zb, src, go_up, go_down):
        if go_up:
            send(both(cond, z + 1 < rows), src, blk(zb, xy), (S_UP, zb), (R_Z, zb), up)
        if go_down:
            send(both(cond, z > 0), src, blk(zb, xy), (S_DN, zb), (R_Z, zb), down)
        send(cond, src, blk(zb, xy), (S_X, zb), (R_X, zb), dev_x)
        send(cond, src, blk(zb, xy), (S_Y, zb), (R_Y, zb), dev_y)

    def state_out(k):
        zt = ring[k]
        send(None, sto.at[0, :, pix(zt)], st.at[core, chan(z)], (S_S, k), (R_S, z), (zt, col))

    def diagonal(cond, zb):
        arrive(cond, blk(zb, xn), (R_X, zb))
        send(cond, blk(zb, xn, 0), blk(zb, xn, 0), (S_D0, zb), (R_D0, zb), dev_y)
        arrive(cond, blk(zb, yn), (R_Y, zb))
        send(cond, blk(zb, yn, 1), blk(zb, yn, 1), (S_D1, zb), (R_D1, zb), dev_x)

    spread(None, z, wown, True, True)
    send(None, sto.at[0, :, pix(z)], st.at[core, chan(z)], (S_F, z), (R_F, z), dev_p)
    for d in range(1, rows + 1):
        if d < rows:
            low, high = z - d, z + d
            arrive(low >= 0, blk(low, xy), (R_Z, low))
            spread(low >= 0, low, blk(low, xy), True, False)
            arrive(high < rows, blk(high, xy), (R_Z, high))
            spread(high < rows, high, blk(high, xy), False, True)
        if d == rows - 2:
            for k in range(1, rows):
                state_out(k)
        if d == rows - 1:
            for k in range(1, rows):
                zt = ring[k]
                send(None, sto.at[1, :, pix(zt)], tg.at[chan(z)], (S_T, k), (R_T, z), (zt, col))
        if d == 1:
            diagonal(None, z)
        else:
            diagonal(z - (d - 1) >= 0, z - (d - 1))
            diagonal(z + (d - 1) < rows, z + (d - 1))
    for k in range(1, rows):
        zb = ring[rows - k]
        arrive(None, st.at[core, chan(zb)], (R_S, zb))
        send(None, st.at[core, chan(zb)], st.at[core, chan(zb)], (S_F, zb), (R_F, zb), dev_p)
    for zb in range(rows):
        arrive(None, blk(zb, dn, 0), (R_D0, zb))
        arrive(None, blk(zb, dn, 1), (R_D1, zb))
    local_w.wait()
    local_s.wait()
    local_t.wait()

    half_rows = w.shape[1] // 2
    for part in range(2):
        at = slice(part * half_rows, (part + 1) * half_rows)
        block = w[0, at, :].astype(jnp.float32)
        colf[at, :] = jnp.broadcast_to(
            jnp.sqrt(1.0 + jnp.sum(block * block, axis=1, keepdims=True)), (half_rows, colf.shape[1])
        )
    total = jnp.zeros((1, w.shape[2]), jnp.float32)
    for part in range(2):
        block = w[1, part * half_rows : (part + 1) * half_rows, :].astype(jnp.float32)
        total = total + jnp.sum(block * block, axis=0, keepdims=True)
    s2[0] = jnp.broadcast_to(total, s2.shape[1:])
    send(None, s2.at[0], s2.at[1], (MISC, 3), (MISC, 4), dev_p)
    for zb in range(rows):
        arrive(None, st.at[1 - core, chan(zb)], (R_F, zb))

    def forward(j):
        @pl.loop(0, 2)
        def _(part):
            at = pl.ds(pl.multiple_of(part * half_rows, 16), half_rows)
            value = jnp.dot(w[0, at, :], st[j], preferred_element_type=jnp.float32)
            value = value / colf[at, :1]
            pre[j, at, :] = value
            hid[j, at, :] = (value * jax.nn.sigmoid(value) * SILU_GAIN * gsel[j, at, :]).astype(jnp.bfloat16)

    def branch_part(j, dst):
        @pl.loop(0, rows)
        def _(zb):
            at = pl.ds(pl.multiple_of(zb * ip, 128), ip)
            dst[at, :] = lax.dot_general(
                w[1, :, at], hid[j], CONTRACT_LEAD, preferred_element_type=jnp.float32
            )

    forward(1 - core)
    branch_part(1 - core, brp)
    send(None, brp, brr, (MISC, 5), (MISC, 6), dev_p)
    forward(core)
    branch_part(core, brk)
    for k in range(1, rows):
        arrive(None, tg.at[chan(ring[k])], (R_T, ring[k]))
    arrive(None, s2.at[1], (MISC, 4))
    col2_row = jnp.sqrt(1.0 + s2[0] + s2[1])
    col2 = col2_row.T[:, :1]
    arrive(None, brr, (MISC, 6))
    for zb in range(rows):
        at = slice(zb * ip, (zb + 1) * ip)
        norm = col2[at, :]
        branch = (brk[at, :] + brr[at, :]) / norm
        fresh = (KEEP_COEF * st[core, at, :].astype(jnp.float32) + ADD_COEF * branch).astype(jnp.bfloat16)
        slope = (fresh.astype(jnp.float32) - tg[at, :].astype(jnp.float32)) / samples
        rounded = (ADD_COEF * slope).astype(jnp.bfloat16)
        dbr[core, at, :] = rounded
        product = jnp.sum(branch * rounded.astype(jnp.float32), axis=1, keepdims=True) * norm
        d2[0, :, at] = jnp.broadcast_to(product, (ip, 128)).T[: d2.shape[1], :]
    send(None, dbr.at[core], dbr.at[core], (MISC, 7), (MISC, 8), dev_p)
    send(None, d2.at[0], d2.at[1], (MISC, 9), (MISC, 10), dev_p)

    def scale_back(j):
        for zb in range(rows):
            at = slice(zb * ip, (zb + 1) * ip)
            db2[j, at, :] = (dbr[j, at, :].astype(jnp.float32) / col2[at, :]).astype(jnp.bfloat16)

    def backward(j):
        @pl.loop(0, 2)
        def _(part):
            at = pl.ds(pl.multiple_of(part * half_rows, 16), half_rows)
            grad = jnp.dot(w[1, at, :], db2[j], preferred_element_type=jnp.float32)
            dpre[j, at, :] = (grad * gsel[j, at, :] * silu_slope(pre[j, at, :]) * SILU_GAIN).astype(jnp.bfloat16)

    scale_back(core)
    backward(core)
    arrive(None, dbr.at[1 - core], (MISC, 8))
    arrive(None, d2.at[1], (MISC, 10))
    scale_back(1 - core)
    backward(1 - core)
    dot1 = colf[:, :1] * sum(
        jnp.sum(dpre[j].astype(jnp.float32) * pre[j], axis=1, keepdims=True) for j in range(CORES)
    )
    lane = lax.broadcasted_iota(jnp.int32, (1, ip), 1)
    line = lax.broadcasted_iota(jnp.int32, (hp, 1), 0)

    def gradients(zb):
        at = pl.ds(pl.multiple_of(zb * ip, 128), ip)
        first = sum(
            lax.dot_general(dpre[j], st[j, at, :], CONTRACT_TAIL, preferred_element_type=jnp.float32)
            for j in range(CORES)
        )
        g[0, :, at] = jnp.where(lane >= ib, dot1, first).astype(jnp.bfloat16)
        second = sum(
            lax.dot_general(hid[j], dbr[j, at, :], CONTRACT_TAIL, preferred_element_type=jnp.float32)
            for j in range(CORES)
        )
        dot2 = d2[0, :1, at] + d2[1, :1, at]
        for b in range(chips):
            part = second[b * hp : (b + 1) * hp, :]
            g[1, b * hp : (b + 1) * hp, at] = jnp.where(line >= hb, dot2, part).astype(jnp.bfloat16)

    def gblk(half, xyb, zb):
        return (half, pl.ds(pl.multiple_of(xyb * hp, 16), hp), pl.ds(pl.multiple_of(zb * ip, 128), ip))

    order = ring[1:] + ring[:1]

    def stage_a(k):
        zb = order[k]
        send(None, g.at[gblk(0, dn, zb)], ra.at[0, k], (S_A0, k), (R_A0, k), dev_y)
        send(None, g.at[gblk(1, dn, zb)], ra.at[1, k], (S_A1, k), (R_A1, k), dev_x)
        send(None, g.at[gblk(1, xn, zb)], rx.at[1, k], (S_CX, k), (R_CX, k), dev_x)
        send(None, g.at[gblk(0, yn, zb)], ry.at[0, k], (S_CY, k), (R_CY, k), dev_y)

    def wide(value):
        return value.astype(jnp.float32)

    def stage_b(k):
        zb = order[k]
        arrive(None, ra.at[0, k], (R_A0, k))
        sa[0, k] = (wide(g[gblk(0, xn, zb)]) + wide(ra[0, k])).astype(jnp.bfloat16)
        send(None, sa.at[0, k], rx.at[0, k], (S_BX, k), (R_BX, k), dev_x)
        arrive(None, ra.at[1, k], (R_A1, k))
        sa[1, k] = (wide(g[gblk(1, yn, zb)]) + wide(ra[1, k])).astype(jnp.bfloat16)
        send(None, sa.at[1, k], ry.at[1, k], (S_BY, k), (R_BY, k), dev_y)

    def stage_c(k):
        zb = order[k]
        arrive(None, rx.at[1, k], (R_CX, k))
        arrive(None, ry.at[0, k], (R_CY, k))
        arrive(None, rx.at[0, k], (R_BX, k))
        arrive(None, ry.at[1, k], (R_BY, k))
        sums = [wide(g[gblk(half, xy, zb)]) + wide(rx[half, k]) + wide(ry[half, k]) for half in range(2)]
        if k == rows - 1:
            return sums
        pz[k, 0] = sums[0].astype(jnp.bfloat16)
        pz[k, 1] = sums[1].astype(jnp.bfloat16)
        send(None, pz.at[k], rz.at[k], (S_P, k), (R_P, k), (zb, col))
        return None

    for k in range(rows):
        gradients(order[k])
        stage_a(k)
        if k >= 1:
            stage_b(k - 1)
    sums = None
    for k in range(rows):
        if k == rows - 2:
            stage_b(rows - 1)
        sums = stage_c(k)
    for k in range(rows - 1):
        arrive(None, rz.at[k], (R_P, k))
    first, second = (
        sums[half] + sum(wide(rz[k, half]) for k in range(rows - 1)) for half in range(2)
    )
    norm1 = colf[pl.ds(pl.multiple_of(xy * hp, 16), hp), :1][:hb]
    dot_first = first[:hb, ib : ib + 1]
    out1[...] = first[:hb, :ib] / norm1 - w1f[...] * (dot_first / (norm1 * norm1 * norm1))
    mine = pl.ds(pl.multiple_of(z * ip, 128), ip)
    norm2 = jnp.sqrt(1.0 + s2[0, :1, mine] + s2[1, :1, mine])[:, :ib]
    dot_second = second[hb : hb + 1, :ib]
    out2[...] = second[:hb, :ib] / norm2 - w2f[...] * (dot_second / (norm2 * norm2 * norm2))
    for cond, spec in pending:
        when(cond, lambda spec=spec: remote(*spec).wait_send())


def local_step(clean, noise, bucket, mod_table, w_first, w_second):
    rows = lax.axis_size("row")
    cols = lax.axis_size("col")
    z, col = lax.axis_index("row"), lax.axis_index("col")
    samples = bucket.shape[0]
    own_rows = clean.shape[1]
    ib, hb = clean.shape[0], w_first.shape[2]
    sub = own_rows // rows
    if sub != PIX:
        return local(clean, noise, bucket, mod_table, w_first, w_second)
    chips = cols // CORES
    hp, ip = round_up(hb + 1, 16), round_up(ib + 1, 128)
    bf16 = jnp.bfloat16
    w1f, w2f = w_first[0].T, w_second[0]
    wown = jnp.stack([w1f, w2f]).astype(bf16)
    wown = jnp.pad(wown, ((0, 0), (0, hp - hb), (0, ip - ib)))
    sample = lax.dynamic_slice_in_dim(bucket, col * rows, rows)
    levels = jnp.repeat(noise_levels(sample), PIX)[None, :]
    root = jnp.sqrt(levels * levels + 0.25)
    sto = jnp.stack([
        ((clean + levels * noise) / root).astype(bf16),
        (clean * (2.0 * levels / root) - noise * (0.5 / root)).astype(bf16),
    ])
    chip = col // CORES
    picked = jnp.stack([lax.dynamic_index_in_dim(bucket, (chip * CORES + j) * rows + z, keepdims=False) for j in range(CORES)])
    table = mod_table[0].reshape(mod_table.shape[1], chips, CORES, hb)
    mine = lax.dynamic_index_in_dim(table, lax.rem(col, CORES), axis=2, keepdims=False)
    gsel = 1.0 + jnp.take(mine, picked, axis=0)
    gsel = jnp.pad(gsel, ((0, 0), (0, 0), (0, hp - hb))).reshape(CORES, chips * hp, 1)
    hh, ii = chips * hp, rows * ip
    f32 = jnp.float32
    vmem = pl.BlockSpec(memory_space=pltpu.VMEM)
    out1, out2 = pl.pallas_call(
        lambda *refs: step_kernel(hb, ib, samples, *refs),
        out_shape=(jax.ShapeDtypeStruct((hb, ib), f32), jax.ShapeDtypeStruct((hb, ib), f32)),
        in_specs=[vmem] * 5,
        out_specs=(vmem, vmem),
        scratch_shapes=[
            pltpu.VMEM((2, hh, ii), bf16),
            pltpu.VMEM((2, ii, sub), bf16),
            pltpu.VMEM((ii, sub), bf16),
            pltpu.VMEM((2, hh, sub), f32),
            pltpu.VMEM((2, hh, sub), bf16),
            pltpu.VMEM((ii, sub), f32),
            pltpu.VMEM((ii, sub), f32),
            pltpu.VMEM((ii, sub), f32),
            pltpu.VMEM((2, ii, sub), bf16),
            pltpu.VMEM((2, ii, sub), bf16),
            pltpu.VMEM((2, hh, sub), bf16),
            pltpu.VMEM((2, 8, ii), f32),
            pltpu.VMEM((2, 8, ii), f32),
            pltpu.VMEM((2, hh, ii), bf16),
            pltpu.VMEM((2, rows, hp, ip), bf16),
            pltpu.VMEM((2, rows, hp, ip), bf16),
            pltpu.VMEM((2, rows, hp, ip), bf16),
            pltpu.VMEM((2, rows, hp, ip), bf16),
            pltpu.VMEM((rows, 2, hp, ip), bf16),
            pltpu.VMEM((rows, 2, hp, ip), bf16),
            pltpu.VMEM((hh, 128), f32),
            pltpu.SemaphoreType.DMA((32, max(rows, 11))),
        ],
        compiler_params=pltpu.CompilerParams(
            collective_id=0, has_side_effects=True, vmem_limit_bytes=60 * 1024 * 1024
        ),
    )(wown, sto, gsel, w1f, w2f)
    return (out1.T[None], out2[None])


def solution(mesh):
    placed = (
        P("row", "col"),
        P("row", "col"),
        P(),
        P(),
        P(None, "row", "col"),
        P(None, "col", "row"),
    )
    return jax.shard_map(
        local_step if mesh.shape["col"] == CORES * SIDE * SIDE else local,
        mesh=mesh,
        in_specs=placed,
        out_specs=(P(None, "row", "col"), P(None, "col", "row")),
        check_vma=False,
    )
```

profile of v0, /device:TPU:0, one launch (start us, length us, event | category | flops | bytes accessed | tf_op | source)
XLA Modules:
  0.0 121.3 jit_solution(15192127045284654312)
XLA Ops:
  0.6 0.7 add_exponential_fusion
  1.4 0.1 broadcast_bitcast_fusion
  1.5 2.2 %fusion.1 = (bf16[1,336,1024]{2,1,0:T(8,128)(2,1)S(1)}, bf16[1,336,1024]{2,1,0:T(8,128)(2,1)S(1)}) fusion(f32[1024]{0:T(1024)S(1)} %get-tuple-element.8, f32[336,1024]{1,0:T(8,128)} %param.6, f32[336,1024]{1,0:T(8,128)} %param.7, f32[1024]{0:T(1024)S(1)} %bitcast.31, f32[1024]{0:T(1024)S(1)} %get-tuple-element.9, f32[1024]{0:T(1024)S(1)} %get-tuple-element.10), kind=kLoop, calls=%fused_computation.5 | loop fusion | flops 2752512 | bytes 4145152 | tf_op jit(solution)/shard_map/stack | solution.py:438
  3.7 0.0 copy-start.3
  3.7 0.0 copy-start.2
  3.7 1.2 %pad_maximum_fusion.refs_1_ = bf16[2,336,1024]{2,1,0:T(8,128)(2,1)} fusion(bf16[1,336,1024]{2,1,0:T(8,128)(2,1)S(1)} %get-tuple-element.7, bf16[1,336,1024]{2,1,0:T(8,128)(2,1)S(1)} %get-tuple-element.6), kind=kLoop, calls=%fused_computation.1 | loop fusion | flops 688128 | bytes 2752512 | tf_op jit(solution)/shard_map/stack | solution.py:438
  4.9 0.0 copy-start
  4.9 0.0 copy-start.1
  4.9 0.0 copy-done.3
  4.9 0.6 fusion.10
  5.5 1.4 %fusion.9 = s32[2]{0:T(128)S(1)} fusion(s32[1,1]{0,1:T(1,128)} %bitcast.6, s32[1,1]{0,1:T(1,128)} %bitcast.5), kind=kLoop, calls=%fused_computation.26 | loop fusion | flops 8 | bytes 16 | tf_op jit(solution)/shard_map/jit(_take)/jit(_where)/select_n | solution.py:446
  6.9 0.0 copy-done.2
  6.9 0.5 reshape_squeeze.3
  7.4 0.1 constant_dynamic-slice_fusion
  7.5 0.6 gather_fusion
  8.1 1.4 %compare_and_fusion = pred[2]{0:T(512)(128)(4,1)S(1)} fusion(s32[1]{0:T(128)} %get-tuple-element.12, s32[1]{0:T(128)} %get-tuple-element.11), kind=kLoop, calls=%fused_computation.25 | loop fusion | flops 14 | bytes 10 | tf_op jit(solution)/shard_map/jit(_take)/and | solution.py:446
  9.5 0.1 select_add_fusion
  9.6 1.2 reshape.139.refs_2_
  10.7 0.0 copy-done
  10.8 0.0 copy-done.1
  10.8 0.7 fusion.7.refs_0_
  11.5 106.4 %shard_map.77 = (f32[168,336]{1,0:T(8,128)}, f32[168,336]{1,0:T(8,128)}) custom-call(bf16[2,176,384]{2,1,0:T(8,128)(2,1)} %fusion.7.refs_0_, bf16[2,336,1024]{2,1,0:T(8,128)(2,1)} %pad_maximum_fusion.refs_1_, f32[2,704,1]{2,1,0:T(8,128)} %reshape.139.refs_2_, f32[168,336]{1,0:T(8,128)} %bitcast.26, f32[168,336]{1,0:T(8,128)} %bitcast.25), custom_call_target="tpu_custom_call" | custom-call | tf_op jit(solution)/shard_map/pallas_call | solution.py:451
  118.0 1.7 %copy.15 = f32[1,336,168]{1,2,0:T(8,128)} copy(f32[1,336,168]{1,2,0:T(8,128)} %bitcast.28) | data formatting | bytes 451584
  119.6 1.7 %copy.16 = f32[1,168,336]{2,1,0:T(8,128)} copy(f32[1,168,336]{2,1,0:T(8,128)} %bitcast.27) | data formatting | bytes 451584
  (7 shorter events, 0.1 us)
Async XLA Ops:
  3.7 1.3 %copy-start.3 = (s32[32]{0:T(128)S(1)}, s32[32]{0:T(128)}, u32[]{:S(2)}) copy-start(s32[32]{0:T(128)} %param.8) | copy-start | bytes 388
  3.7 3.2 %copy-start.2 = (f32[1,32,1344]{2,1,0:T(8,128)S(1)}, f32[1,32,1344]{2,1,0:T(8,128)}, u32[]{:S(2)}) copy-start(f32[1,32,1344]{2,1,0:T(8,128)} %param.9) | copy-start | bytes 516100
  4.9 5.8 %copy-start = (f32[1,168,336]{2,1,0:T(8,128)S(1)}, f32[1,168,336]{2,1,0:T(8,128)}, u32[]{:S(2)}) copy-start(f32[1,168,336]{2,1,0:T(8,128)} %param.11) | copy-start | bytes 677380
  4.9 5.8 %copy-start.1 = (f32[1,336,168]{1,2,0:T(8,128)S(1)}, f32[1,336,168]{1,2,0:T(8,128)}, u32[]{:S(2)}) copy-start(f32[1,336,168]{1,2,0:T(8,128)} %param.10) | copy-start | bytes 677380
where the time goes:
time: 122 us; the launch traced here: 121 us
  Pallas kernels  106 us (87%)
  other arithmetic  7.77 us (6%)
  local copies, waits for them, and re-layouts  6.38 us (5%)
    pallas_call x1, Pallas kernels, local_step(): pl.pallas_call(lambda *refs: step_kernel(hb, ib, samples, *refs), out_sha...  106 us
    unnamed x13, local copies, waits for them, and re-layouts  3.46 us
    another operation x2, other arithmetic, local_step(): jnp.stack([((clean + levels * noise) / root).astype(bf16), (clean * (2.0...  3.41 us

commit v1 on v0

v1 whole, which is shorter than its diff:
```python
import math

import jax
import jax.numpy as jnp
from jax import lax
from jax.experimental import pallas as pl
from jax.experimental.pallas import tpu as pltpu
from jax.sharding import PartitionSpec as P

PIX = 256
BUCKETS = 32


MIX_WEIGHT = 0.3
KEEP_COEF = (1.0 - MIX_WEIGHT) / math.sqrt((1.0 - MIX_WEIGHT) ** 2 + MIX_WEIGHT**2)
ADD_COEF = MIX_WEIGHT / math.sqrt((1.0 - MIX_WEIGHT) ** 2 + MIX_WEIGHT**2)
SILU_GAIN = 1.0 / 0.596
CONTRACT_LEAD = (((0,), (0,)), ((), ()))
CONTRACT_TAIL = (((1,), (1,)), ((), ()))


def noise_levels(bucket):
    return jnp.exp(-3.0 + 5.0 * (bucket.astype(jnp.float32) + 0.5) / BUCKETS)


def silu_slope(values):
    sig = jax.nn.sigmoid(values)
    return sig * (1.0 + values * (1.0 - sig))


def bucket_gains(table, picked):
    onehot = (picked[:, None] == jnp.arange(table.shape[0], dtype=jnp.int32)[None, :]).astype(
        jnp.float32
    )
    return jnp.dot(
        onehot, table, precision=lax.Precision.HIGHEST, preferred_element_type=jnp.float32
    )


def local(clean, noise, bucket, mod_table, w_first, w_second):
    rows_size = lax.axis_size("row")
    row_at = lax.axis_index("row")
    col_at = lax.axis_index("col")
    samples = bucket.shape[0]
    own_rows = clean.shape[1]
    weight_first = w_first[0]
    weight_second = w_second[0]
    table = 1.0 + mod_table[0]
    col_first = jnp.sqrt(lax.psum(jnp.sum(weight_first * weight_first, axis=0), "row") + 1.0)
    col_second = jnp.sqrt(lax.psum(jnp.sum(weight_second * weight_second, axis=0), "col") + 1.0)
    normed_first = (weight_first / col_first[None, :]).astype(jnp.bfloat16)
    normed_second = (weight_second / col_second[None, :]).astype(jnp.bfloat16)
    chan_clean, chan_noise = (
        lax.all_to_all(
            clean.astype(jnp.bfloat16), "row", split_axis=1, concat_axis=0, tiled=True
        ).astype(clean.dtype),
        lax.all_to_all(
            noise.astype(jnp.bfloat16), "row", split_axis=1, concat_axis=0, tiled=True
        ).astype(noise.dtype),
    )
    local_clean = chan_clean.T
    local_noise = chan_noise.T
    sub_rows = own_rows // rows_size
    first_row = col_at * own_rows + row_at * sub_rows
    row_sample = (first_row + jnp.arange(sub_rows, dtype=jnp.int32)) // PIX
    row_bucket = jnp.take(bucket, row_sample)
    levels = noise_levels(row_bucket)[:, None]
    spread_root = jnp.sqrt(levels * levels + 0.25)
    state_own = ((local_clean + levels * local_noise) / spread_root).astype(jnp.bfloat16)
    target = local_clean * (2.0 * levels / spread_root) - local_noise * (0.5 / spread_root)
    gains = bucket_gains(table, row_bucket)
    part_first, part_second = (
        lax.all_gather(normed_first, "col", axis=1, tiled=True),
        lax.all_gather(normed_second, "col", axis=0, tiled=True),
    )
    full_first, full_second = (
        lax.all_gather(part_first, "row", axis=0, tiled=True),
        lax.all_gather(part_second, "row", axis=1, tiled=True),
    )
    pre_act = jnp.dot(state_own, full_first, preferred_element_type=jnp.float32)
    hidden = (jax.nn.silu(pre_act) * SILU_GAIN * gains).astype(jnp.bfloat16)
    branch = jnp.dot(hidden, full_second, preferred_element_type=jnp.float32)
    state_new = (KEEP_COEF * state_own.astype(jnp.float32) + ADD_COEF * branch).astype(jnp.bfloat16)
    grad_own = (state_new.astype(jnp.float32) - target) / samples
    dbranch = (ADD_COEF * grad_own).astype(jnp.bfloat16)
    gsecond_full = lax.dot_general(
        hidden, dbranch, CONTRACT_LEAD, preferred_element_type=jnp.float32
    )
    dhidden = lax.dot_general(
        dbranch, full_second, CONTRACT_TAIL, preferred_element_type=jnp.float32
    )
    dpre = (dhidden * gains * silu_slope(pre_act) * SILU_GAIN).astype(jnp.bfloat16)
    gfirst_full = lax.dot_general(
        state_own, dpre, CONTRACT_LEAD, preferred_element_type=jnp.float32
    )
    part_gfirst, part_gsecond = (
        lax.psum_scatter(
            gfirst_full.astype(jnp.bfloat16), "col", scatter_dimension=1, tiled=True
        ).astype(jnp.float32),
        lax.psum_scatter(
            gsecond_full.astype(jnp.bfloat16), "col", scatter_dimension=0, tiled=True
        ).astype(jnp.float32),
    )
    gfirst, gsecond = (
        lax.psum_scatter(
            part_gfirst.astype(jnp.bfloat16), "row", scatter_dimension=0, tiled=True
        ).astype(jnp.float32),
        lax.psum_scatter(
            part_gsecond.astype(jnp.bfloat16), "row", scatter_dimension=1, tiled=True
        ).astype(jnp.float32),
    )
    dot_first = lax.psum(jnp.sum(weight_first * gfirst, axis=0), "row")
    dot_second = lax.psum(jnp.sum(weight_second * gsecond, axis=0), "col")
    grad_first = gfirst / col_first[None, :] - weight_first * (dot_first / col_first**3)[None, :]
    grad_second = (
        gsecond / col_second[None, :] - weight_second * (dot_second / col_second**3)[None, :]
    )
    return (grad_first[None], grad_second[None])


CORES = 2
SIDE = 2
MESH = pl.DeviceIdType.MESH


def round_up(size, unit):
    return -(-size // unit) * unit


def twice(value):
    return jnp.concatenate([value, value], axis=1)


def split_sum(total):
    high = total.astype(jnp.bfloat16)
    low = (total - high.astype(jnp.float32)).astype(jnp.bfloat16)
    return high, low


def step_kernel(
    hb, ib, samples, names, bucket, clean, noise, table, w1h, w2h, out1, out2,
    cl, no, w1f, w2f, sto, w, st, tg, nrm, gain, pre, slp, hid, brk, brp, brr, dbr, db2, dpre,
    s2, d2, dot1, g, ra, sa, rb, rc, pz, rz, sems, local_sems,
):
    rows = st.shape[0] // round_up(ib + 1, 128)
    hp, ip = round_up(hb + 2, 16), round_up(ib + 1, 128)
    chips = w.shape[1] // hp
    sub = tg.shape[1]
    hh, ii = chips * hp, rows * ip
    own_rows = cl.shape[1]
    bf16, f32 = jnp.bfloat16, jnp.float32
    z = lax.axis_index("row")
    col = lax.axis_index("col")
    core = lax.rem(col, CORES)
    xy = col // CORES
    x, y = lax.rem(xy, SIDE), xy // SIDE
    xn = y * SIDE + (1 - x)
    yn = (1 - y) * SIDE + x
    dn = (1 - y) * SIDE + (1 - x)
    dev_x = (z, xn * CORES + core)
    dev_y = (z, yn * CORES + core)
    dev_p = (z, xy * CORES + 1 - core)
    up, down = (z + 1, col), (z - 1, col)
    ring = [lax.rem(z + k, rows) for k in range(rows)]
    side = 1 - 2 * (z // (rows // 2))
    near = [z] + [lax.rem(z + side * k + rows, rows) for k in range(1, rows)]

    loads = []
    for k, (src, dst) in enumerate([(w1h, w1f), (w2h, w2f), (clean, cl), (noise, no)]):
        loads.append(pltpu.make_async_copy(src, dst, local_sems.at[k]))
        loads[-1].start()
    barrier = pltpu.get_barrier_semaphore()
    peers = [dev_x, dev_y, dev_p] + [(ring[k], col) for k in range(1, rows)]
    for peer in peers:
        pl.semaphore_signal(barrier, inc=1, device_id=peer, device_id_type=MESH)

    pending = []

    def sem(kind, at):
        return sems.at[names.setdefault(kind, len(names)), at]

    def remote(src, dst, kind, at_send, at_recv, dev):
        return pltpu.make_async_remote_copy(
            src_ref=src, dst_ref=dst, send_sem=sem("s" + kind, at_send),
            recv_sem=sem("r" + kind[:2], at_recv), device_id=dev, device_id_type=MESH,
        )

    def when(cond, fn):
        if cond is None:
            fn()
        else:
            pl.when(cond)(fn)

    def send(cond, *spec):
        when(cond, lambda: remote(*spec).start())
        pending.append((cond, spec))

    def arrive(cond, dst, kind, at):
        flag = sem("r" + kind, at)
        when(cond, lambda: pltpu.make_async_remote_copy(
            src_ref=dst, dst_ref=dst, send_sem=flag, recv_sem=flag, device_id=dev_p, device_id_type=MESH,
        ).wait_recv())

    def span(start, size, unit):
        return pl.ds(pl.multiple_of(start, unit), size)

    def cut(m):
        return round_up(hp // 2, 16) if m == 0 else hp - round_up(hp // 2, 16)

    def part_rows(m, p):
        return (0, cut(m)) if p == 0 else (cut(m), hp - cut(m))

    def wblk(m, xyb, zb, p=None):
        lo, size = (0, hp) if p is None else part_rows(m, p)
        return w.at[m, span(xyb * hp + lo, size, 16), span(zb * ip, ip, 128)]

    def chan(zb, size=ib):
        return span(zb * ip, size, 16)

    def pix(zb):
        return span(zb * sub, sub, 128)

    mine, other = slice(0, sub), slice(sub, 2 * sub)

    for zb in range(rows):
        pad = slice(zb * ip + ib, (zb + 1) * ip)
        st[pad, :] = jnp.zeros((ip - ib, 2 * sub), bf16)
        tg[pad, :] = jnp.zeros((ip - ib, sub), bf16)

    line = lax.broadcasted_iota(jnp.int32, (hp, ip), 0)
    for m, full in enumerate((w1f, w2f)):
        loads[m].wait()
        block = jnp.pad(full[...], ((0, hp - hb), (0, ip - ib)))
        if m == 0:
            total = jnp.sum(block * block, axis=1, keepdims=True)
            total = jnp.pad(jnp.broadcast_to(total, (hp, 128)), ((0, 256 - hp), (0, 0)))
            total = jnp.pad(total.T[:1, :], ((0, 0), (0, ip - 256)))
        else:
            total = jnp.sum(block * block, axis=0, keepdims=True)
        high, low = split_sum(total)
        block = jnp.where(line == hb, high.astype(f32), block)
        block = jnp.where(line == hb + 1, low.astype(f32), block)
        w[m, span(xy * hp, hp, 16), span(z * ip, ip, 128)] = block.astype(bf16)
    pl.semaphore_wait(barrier, len(peers))

    def along_z(cond, m, zb, go_up, go_down):
        if go_up:
            send(both(cond, z + 1 < rows), wblk(m, xy, zb), wblk(m, xy, zb), f"z{m}u", zb, zb, up)
        if go_down:
            send(both(cond, z > 0), wblk(m, xy, zb), wblk(m, xy, zb), f"z{m}d", zb, zb, down)

    def both(a, b):
        return b if a is None else jnp.logical_and(a, b)

    def across(cond, m, zb):
        send(cond, wblk(m, xy, zb), wblk(m, xy, zb), f"x{m}", zb, zb, dev_x)
        send(cond, wblk(m, xy, zb), wblk(m, xy, zb), f"y{m}", zb, zb, dev_y)

    def diagonal(cond, m, zb):
        arrive(cond, wblk(m, xn, zb), f"x{m}", zb)
        send(cond, wblk(m, xn, zb, 0), wblk(m, xn, zb, 0), f"a{m}", zb, zb, dev_y)
        arrive(cond, wblk(m, yn, zb), f"y{m}", zb)
        send(cond, wblk(m, yn, zb, 1), wblk(m, yn, zb, 1), f"b{m}", zb, zb, dev_x)

    def sides(d):
        return ((z - d >= 0, z - d, True, False), (z + d < rows, z + d, False, True))

    def hop(m, d):
        for cond, zb, go_up, go_down in sides(d):
            arrive(cond, wblk(m, xy, zb), f"z{m}", zb)
            along_z(cond, m, zb, go_up and d < rows - 1, go_down and d < rows - 1)

    def each_side(fn, m, d):
        if d == 0:
            fn(None, m, z)
        else:
            for cond, zb, _, _ in sides(d):
                fn(cond, m, zb)

    for m in range(2):
        along_z(None, m, z, True, True)
    for m in range(2):
        across(None, m, z)

    loads[2].wait()
    loads[3].wait()
    for k in range(rows):
        lanes = slice(k * sub, (k + 1) * sub)
        picked = jnp.full((1, sub), bucket[col * rows + k], jnp.int32)
        level = noise_levels(picked)
        root = jnp.sqrt(level * level + 0.25)
        c, n = cl[:, lanes], no[:, lanes]
        sto[0, :, lanes] = ((c + level * n) / root).astype(bf16)
        sto[1, :, lanes] = (c * (2.0 * level / root) - n * (0.5 / root)).astype(bf16)
    st[chan(z), mine] = sto[0, :, pix(z)]
    tg[chan(z), :] = sto[1, :, pix(z)]

    def state_to_partner(zb):
        send(None, st.at[chan(zb), mine], st.at[chan(zb), other], "f", zb, zb, dev_p)

    hop(0, 1)
    each_side(across, 0, 1)
    each_side(diagonal, 0, 0)
    hop(1, 1)
    for k in range(1, rows):
        send(None, sto.at[0, :, pix(ring[k])], st.at[chan(z), mine], "t", k, z, (ring[k], col))
    state_to_partner(z)
    each_side(diagonal, 1, 0)
    if rows > 2:
        hop(0, 2)
        each_side(across, 0, 2)
    each_side(across, 1, 1)
    each_side(diagonal, 0, 1)
    if rows > 2:
        hop(1, 2)
    for k in range(1, rows):
        zt = near[k]
        send(None, sto.at[1, :, pix(zt)], tg.at[chan(z), :], "g", k, z, (zt, col))
    for d in range(3, rows):
        hop(0, d)
        each_side(across, 0, d)
    if rows > 2:
        each_side(diagonal, 0, 2)
    each_side(diagonal, 1, 1)
    for d in range(3, rows):
        hop(1, d)
    for d in range(2, rows):
        each_side(across, 1, d)
    stack = []
    for j in range(CORES):
        whose = core if j == 0 else 1 - core
        picked = bucket[(xy * CORES + whose) * rows + z]
        row = 1.0 + table[pl.ds(picked, 1), :]
        for b in range(chips):
            pieces = [row[:, (b * CORES + c) * hb : (b * CORES + c + 1) * hb] for c in range(CORES)]
            piece = jnp.where(core == 0, pieces[0], pieces[1])
            stack.append(jnp.pad(piece, ((0, 0), (0, 256 - hb))))
    for k in range(1, rows):
        zb = ring[rows - k]
        arrive(None, st.at[chan(zb), mine], "t", zb)
        state_to_partner(zb)
    for d in range(3, rows):
        each_side(diagonal, 0, d)
    for zb in range(rows):
        arrive(None, wblk(0, dn, zb, 0), "a0", zb)
        arrive(None, wblk(0, dn, zb, 1), "b0", zb)

    def sums_of(m, b, lanes):
        tail = w[m, (b + 1) * hp - 16 : (b + 1) * hp, lanes].astype(f32)
        at = hb - (hp - 16)
        return tail[at : at + 1, :] + tail[at + 1 : at + 2, :]

    for b in range(chips):
        stack.append(sum(sums_of(0, b, slice(zb * ip, zb * ip + 256)) for zb in range(rows)))
    filler = 128 - len(stack)
    columns = jnp.concatenate(stack + [jnp.zeros((filler, 256), f32)], axis=0).T
    for b in range(chips):
        at = slice(b * hp, (b + 1) * hp)
        for j in range(CORES):
            k = j * chips + b
            gain[j, at, :] = jnp.broadcast_to(columns[:hp, k : k + 1], (hp, 128))
        k = CORES * chips + b
        nrm[at, :] = jnp.broadcast_to(jnp.sqrt(1.0 + columns[:hp, k : k + 1]), (hp, 128))
    for zb in range(rows):
        arrive(None, st.at[chan(zb), other], "f", zb)

    half_rows = hh // 2

    def forward(part):
        at = slice(part * half_rows, (part + 1) * half_rows)
        value = jnp.dot(w[0, at, :], st[...], preferred_element_type=f32)
        inverse = twice(1.0 / nrm[at, :])
        for j in range(CORES):
            lanes = slice(j * sub, (j + 1) * sub)
            v = value[:, lanes] * inverse
            sig = jax.nn.sigmoid(v)
            scale = twice(gain[j, at, :]) * SILU_GAIN
            pre[at, lanes] = v
            hid[at, lanes] = (v * sig * scale).astype(bf16)
            slp[at, lanes] = sig * (1.0 + v * (1.0 - sig)) * scale

    forward(0)
    if rows > 2:
        each_side(diagonal, 1, 2)
    forward(1)
    for d in range(3, rows):
        each_side(diagonal, 1, d)

    def zlanes(zb):
        return span(zb * ip, ip, 128)

    def branch_part(i):
        zb = near[i]
        at = zlanes(zb)
        arrive(None, wblk(1, dn, zb, 0), "a1", zb)
        arrive(None, wblk(1, dn, zb, 1), "b1", zb)
        total = sum(sums_of(1, b, at) for b in range(chips))
        s2[0, :, at] = jnp.broadcast_to(total, (s2.shape[1], ip))
        send(None, s2.at[0, :, at], s2.at[1, :, at], "n", i, zb, dev_p)
        full = lax.dot_general(w[1, :, at], hid[...], CONTRACT_LEAD, preferred_element_type=f32)
        brp[at, :] = full[:, other]
        send(None, brp.at[at, :], brr.at[at, :], "p", i, zb, dev_p)
        brk[at, :] = full[:, mine]

    def slope_part(i):
        zb = near[i]
        at = zlanes(zb)
        if i > 0:
            arrive(None, tg.at[chan(zb), :], "g", zb)
        arrive(None, s2.at[1, :, at], "n", zb)
        total = 1.0 + s2[0, :1, at] + s2[1, :1, at]
        norm = jnp.sqrt(jnp.broadcast_to(total, (128, ip)).T)
        inverse = 1.0 / norm
        arrive(None, brr.at[at, :], "p", zb)
        branch = (brk[at, :] + brr[at, :]) * twice(inverse)
        fresh = (KEEP_COEF * st[at, mine].astype(f32) + ADD_COEF * branch).astype(bf16)
        slope = (fresh.astype(f32) - tg[at, :].astype(f32)) / samples
        rounded = (ADD_COEF * slope).astype(bf16)
        dbr[at, mine] = rounded
        send(None, dbr.at[at, mine], dbr.at[at, other], "q", i, zb, dev_p)
        wide_rounded = rounded.astype(f32)
        db2[at, mine] = (wide_rounded * twice(inverse)).astype(bf16)
        product = jnp.sum(branch * wide_rounded, axis=1, keepdims=True) * norm
        d2[0, :, at] = product.T[: d2.shape[1], :]
        send(None, d2.at[0, :, at], d2.at[1, :, at], "d", i, zb, dev_p)

    hidden_line = lax.broadcasted_iota(jnp.int32, (hp, 1), 0)

    def second_part(i):
        zb = near[i]
        at = zlanes(zb)
        arrive(None, dbr.at[at, other], "q", zb)
        arrive(None, d2.at[1, :, at], "d", zb)
        second = lax.dot_general(hid[...], dbr[at, :], CONTRACT_TAIL, preferred_element_type=f32)
        dot2 = d2[0, :1, at] + d2[1, :1, at]
        for b in range(chips):
            part = second[b * hp : (b + 1) * hp, :]
            g[1, b * hp : (b + 1) * hp, at] = jnp.where(hidden_line >= hb, dot2, part).astype(bf16)
        total = jnp.broadcast_to(1.0 + s2[0, :1, at] + s2[1, :1, at], (128, ip))
        inverse = 1.0 / jnp.sqrt(total.T)
        db2[at, other] = (dbr[at, other].astype(f32) * twice(inverse)).astype(bf16)

    def backward():
        for part in range(2):
            at = slice(part * half_rows, (part + 1) * half_rows)
            grad = jnp.dot(w[1, at, :], db2[...], preferred_element_type=f32)
            rounded = (grad * slp[at, :]).astype(bf16)
            dpre[at, :] = rounded
            total = jnp.sum(rounded.astype(f32) * pre[at, :], axis=1, keepdims=True)
            dot1[at, :] = total * nrm[at, :]

    lane = lax.broadcasted_iota(jnp.int32, (1, ip), 1)
    last = [ring[k] for k in range(1, rows)] + [z]
    orders = (last, near)

    def first_part(i):
        zb = last[i]
        at = zlanes(zb)
        first = lax.dot_general(dpre[...], st[at, :], CONTRACT_TAIL, preferred_element_type=f32)
        g[0, :, at] = jnp.where(lane >= ib, dot1[:, :1], first).astype(bf16)

    def gblk(m, xyb, zb, p):
        lo, size = part_rows(m, p)
        return (m, span(xyb * hp + lo, size, 16), span(zb * ip, ip, 128))

    def rblk(ref, m, i, p):
        lo, size = part_rows(m, p)
        return ref.at[m, i, slice(lo, lo + size), :]

    def legs(p):
        return (yn, dev_y, xn, dev_x) if p == 0 else (xn, dev_x, yn, dev_y)

    def stage_a(m, i):
        zb = orders[m][i]
        for p in range(2):
            nb1, dev1, nb2, dev2 = legs(p)
            send(None, g.at[gblk(m, dn, zb, p)], rblk(ra, m, i, p), f"{'AB'[p]}{m}", i, i, dev1)
        for p in range(2):
            nb1, dev1, nb2, dev2 = legs(p)
            send(None, g.at[gblk(m, nb1, zb, p)], rblk(rc, m, i, p), f"{'CD'[p]}{m}", i, i, dev1)

    def stage_b(m, i):
        zb = orders[m][i]
        for p in range(2):
            nb1, dev1, nb2, dev2 = legs(p)
            arrive(None, rblk(ra, m, i, p), f"{'AB'[p]}{m}", i)
            lo, size = part_rows(m, p)
            inside = (m, i, slice(lo, lo + size))
            sa[inside] = (g[gblk(m, nb2, zb, p)].astype(f32) + ra[inside].astype(f32)).astype(bf16)
            send(None, rblk(sa, m, i, p), rblk(rb, m, i, p), f"{'EF'[p]}{m}", i, i, dev2)

    def stage_c(m, i):
        zb = orders[m][i]
        for p in range(2):
            arrive(None, rblk(rc, m, i, p), f"{'CD'[p]}{m}", i)
            arrive(None, rblk(rb, m, i, p), f"{'EF'[p]}{m}", i)
        own = g[m, span(xy * hp, hp, 16), span(zb * ip, ip, 128)].astype(f32)
        total = own + rb[m, i].astype(f32) + rc[m, i].astype(f32)
        own_at = rows - 1 if m == 0 else 0
        if i == own_at:
            return total
        pz[m, i] = total.astype(bf16)
        send(None, pz.at[m, i], rz.at[m, z], f"P{m}", i, z, (zb, col))
        return None

    sums = [None, None]
    branch_part(0)
    branch_part(1)
    slope_part(0)
    branch_part(2)
    slope_part(1)
    second_part(0)
    stage_a(1, 0)
    branch_part(3)
    second_part(1)
    stage_a(1, 1)
    stage_b(1, 0)
    slope_part(2)
    second_part(2)
    stage_a(1, 2)
    stage_b(1, 1)
    slope_part(3)
    second_part(3)
    stage_a(1, 3)
    sums[1] = stage_c(1, 0)
    stage_b(1, 2)
    backward()
    stage_b(1, 3)
    first_part(0)
    stage_a(0, 0)
    stage_c(1, 1)
    first_part(1)
    stage_a(0, 1)
    stage_c(1, 2)
    stage_b(0, 0)
    first_part(2)
    stage_a(0, 2)
    stage_c(1, 3)
    stage_b(0, 1)
    first_part(3)
    stage_a(0, 3)
    stage_c(0, 0)
    stage_b(0, 2)
    stage_c(0, 1)
    stage_b(0, 3)
    for k in range(1, rows):
        arrive(None, rz.at[1, ring[k]], "P1", ring[k])
    second = sums[1]
    norm2 = jnp.sqrt(1.0 + s2[0, :1, zlanes(z)] + s2[1, :1, zlanes(z)])[:, :ib]
    for k in range(1, rows):
        second = second + rz[1, ring[k]].astype(f32)
    dot_second = second[hb : hb + 1, :ib]
    out2[...] = second[:hb, :ib] / norm2 - w2f[...] * (dot_second / (norm2 * norm2 * norm2))
    stage_c(0, 2)
    first = stage_c(0, 3)
    for k in range(1, rows):
        arrive(None, rz.at[0, ring[k]], "P0", ring[k])
        first = first + rz[0, ring[k]].astype(f32)
    norm1 = nrm[span(xy * hp, hp, 16), :1][:hb]
    dot_first = first[:hb, ib : ib + 1]
    out1[...] = first[:hb, :ib] / norm1 - w1f[...] * (dot_first / (norm1 * norm1 * norm1))
    for cond, spec in pending:
        when(cond, lambda spec=spec: remote(*spec).wait_send())
    assert len(names) <= sems.shape[0], len(names)


def local_step(clean, noise, bucket, mod_table, w_first, w_second):
    rows = lax.axis_size("row")
    cols = lax.axis_size("col")
    samples = bucket.shape[0]
    own_rows = clean.shape[1]
    ib, hb = clean.shape[0], w_first.shape[2]
    sub = own_rows // rows
    if sub != PIX or rows != 4:
        return local(clean, noise, bucket, mod_table, w_first, w_second)
    chips = cols // CORES
    hp, ip = round_up(hb + 2, 16), round_up(ib + 1, 128)
    bf16, f32 = jnp.bfloat16, jnp.float32
    hh, ii = chips * hp, rows * ip
    vmem = pl.BlockSpec(memory_space=pltpu.VMEM)
    smem = pl.BlockSpec(memory_space=pltpu.SMEM)
    anywhere = pl.BlockSpec(memory_space=pl.ANY)
    out1, out2 = pl.pallas_call(
        lambda *refs: step_kernel(hb, ib, samples, {}, *refs),
        out_shape=(jax.ShapeDtypeStruct((hb, ib), f32), jax.ShapeDtypeStruct((hb, ib), f32)),
        in_specs=[smem, anywhere, anywhere, vmem, anywhere, anywhere],
        out_specs=(vmem, vmem),
        scratch_shapes=[
            pltpu.VMEM((ib, own_rows), f32),
            pltpu.VMEM((ib, own_rows), f32),
            pltpu.VMEM((hb, ib), f32),
            pltpu.VMEM((hb, ib), f32),
            pltpu.VMEM((2, ib, own_rows), bf16),
            pltpu.VMEM((2, hh, ii), bf16),
            pltpu.VMEM((ii, CORES * sub), bf16),
            pltpu.VMEM((ii, sub), bf16),
            pltpu.VMEM((hh, 128), f32),
            pltpu.VMEM((CORES, hh, 128), f32),
            pltpu.VMEM((hh, CORES * sub), f32),
            pltpu.VMEM((hh, CORES * sub), f32),
            pltpu.VMEM((hh, CORES * sub), bf16),
            pltpu.VMEM((ii, sub), f32),
            pltpu.VMEM((ii, sub), f32),
            pltpu.VMEM((ii, sub), f32),
            pltpu.VMEM((ii, CORES * sub), bf16),
            pltpu.VMEM((ii, CORES * sub), bf16),
            pltpu.VMEM((hh, CORES * sub), bf16),
            pltpu.VMEM((2, 8, ii), f32),
            pltpu.VMEM((2, 8, ii), f32),
            pltpu.VMEM((hh, 128), f32),
            pltpu.VMEM((2, hh, ii), bf16),
            pltpu.VMEM((2, rows, hp, ip), bf16),
            pltpu.VMEM((2, rows, hp, ip), bf16),
            pltpu.VMEM((2, rows, hp, ip), bf16),
            pltpu.VMEM((2, rows, hp, ip), bf16),
            pltpu.VMEM((2, rows, hp, ip), bf16),
            pltpu.VMEM((2, rows, hp, ip), bf16),
            pltpu.SemaphoreType.DMA((80, rows)),
            pltpu.SemaphoreType.DMA((4,)),
        ],
        compiler_params=pltpu.CompilerParams(
            collective_id=0, has_side_effects=True, vmem_limit_bytes=60 * 1024 * 1024
        ),
    )(bucket, clean, noise, mod_table[0], w_first[0].T, w_second[0])
    return (out1.T[None], out2[None])


def solution(mesh):
    placed = (
        P("row", "col"),
        P("row", "col"),
        P(),
        P(),
        P(None, "row", "col"),
        P(None, "col", "row"),
    )
    return jax.shard_map(
        local_step if mesh.shape["col"] == CORES * SIDE * SIDE else local,
        mesh=mesh,
        in_specs=placed,
        out_specs=(P(None, "row", "col"), P(None, "col", "row")),
        check_vma=False,
    )
```

time: 122 us -> 103 us (0.84)
  other arithmetic: 7.77 us -> 0 us
  Pallas kernels: 106 us -> 99 us
  local copies, waits for them, and re-layouts: 6.38 us -> 3.32 us
    pallas_call x1, Pallas kernels: 106 us -> 99 us  [local_step(): pl.pallas_call(lambda *refs: step_kernel(hb, ib, samples, {}, *refs), out...]
    another operation x5 -> x0, other arithmetic: 4.19 us -> none  [the longest x2 3.41 us: local_step(): jnp.stack([((clean + levels * noise) / root).astype(bf16), (clean * (2.0...]
    and x1 -> x0, other arithmetic: 1.37 us -> none  [local_step(): gsel = 1.0 + jnp.take(mine, picked, axis=0)]
    select_n x1 -> x0, other arithmetic: 1.37 us -> none  [local_step(): gsel = 1.0 + jnp.take(mine, picked, axis=0)]
    unnamed x13 -> x2, local copies, waits for them, and re-layouts: 3.46 us -> 3.32 us
where the time goes in v1:
time: 103 us
  Pallas kernels  99 us (96%)
  local copies, waits for them, and re-layouts  3.32 us (3%)
    pallas_call x1, Pallas kernels, local_step(): pl.pallas_call(lambda *refs: step_kernel(hb, ib, samples, {}, *refs), out...  99 us
    unnamed x2, local copies, waits for them, and re-layouts  3.32 us

profile of v1, /device:TPU:0, one launch (start us, length us, event | category | flops | bytes accessed | tf_op | source)
XLA Modules:
  0.0 102.9 jit_solution(16132971083699002770)
XLA Ops:
  0.6 99.0 %shard_map.77 = (f32[168,336]{1,0:T(8,128)}, f32[168,336]{1,0:T(8,128)}) custom-call(s32[32]{0:T(128)} %refs_0_.1, f32[336,1024]{1,0:T(8,128)} %refs_1_.1, f32[336,1024]{1,0:T(8,128)} %refs_2_.1, f32[32,1344]{1,0:T(8,128)} %bitcast.13, f32[168,336]{1,0:T(8,128)} %bitcast.9, f32[168,336]{1,0:T(8,128)} %bitcast.10), custom_call_target="tpu_custom_call" | custom-call | tf_op jit(solution)/shard_map/pallas_call | solution.py:583
  99.6 1.7 %copy.10 = f32[1,336,168]{1,2,0:T(8,128)} copy(f32[1,336,168]{1,2,0:T(8,128)} %bitcast.12) | data formatting | bytes 451584
  101.3 1.7 %copy.11 = f32[1,168,336]{2,1,0:T(8,128)} copy(f32[1,168,336]{2,1,0:T(8,128)} %bitcast.11) | data formatting | bytes 451584

commit v2 on v1

--- a/solution.py
+++ b/solution.py
@@ -131,6 +131,21 @@
     return jnp.concatenate([value, value], axis=1)
 
 
+def packing(hb, ib):
+    full = ib // 128 * 128
+    carried = round_up(ib + 1, 128) - ib
+    left = ib - full - carried
+    group = round_up(-(-round_up(hb + 2, 16) * max(left, 1) // 128), 16)
+    return full, carried, left, group
+
+
+SINGLE = set(
+    [f"s{kind}{m}" for kind in "abABCDEFPxy" for m in range(2)]
+    + ["s" + kind for kind in "ftgpqnd"] + ["ra0", "rb0", "rP0", "rP1"]
+    + ["sz_z00", "sz_z01", "sz_z1"]
+)
+
+
 def split_sum(total):
     high = total.astype(jnp.bfloat16)
     low = (total - high.astype(jnp.float32)).astype(jnp.bfloat16)
@@ -138,16 +153,20 @@
 
 
 def step_kernel(
-    hb, ib, samples, names, bucket, clean, noise, table, w1h, w2h, out1, out2,
-    cl, no, w1f, w2f, sto, w, st, tg, nrm, gain, pre, slp, hid, brk, brp, brr, dbr, db2, dpre,
-    s2, d2, dot1, g, ra, sa, rb, rc, pz, rz, sems, local_sems,
+    hb, ib, samples, names, bucket, clean, noise, table, w1h, w2h, out1h, out2h,
+    cl, no, w1f, w2f, sto, w, wt, st, tg, nrm, gain, pre, slp, hid, brk, brp, brr, dbr, db2, dpre,
+    s2, d2, dot1, g, gt, ra0, ra1, sa0, sa1, rb0, rb1, rc0, rc1, pz0, pz1, rz0, rz1, out1, out2,
+    sems, local_sems,
 ):
+    ra, sa, rb, rc, pz, rz = (ra0, ra1), (sa0, sa1), (rb0, rb1), (rc0, rc1), (pz0, pz1), (rz0, rz1)
     rows = st.shape[0] // round_up(ib + 1, 128)
     hp, ip = round_up(hb + 2, 16), round_up(ib + 1, 128)
     chips = w.shape[1] // hp
     sub = tg.shape[1]
     hh, ii = chips * hp, rows * ip
     own_rows = cl.shape[1]
+    full, carried, left, group = packing(hb, ib)
+    tp = wt.shape[2]
     bf16, f32 = jnp.bfloat16, jnp.float32
     z = lax.axis_index("row")
     col = lax.axis_index("col")
@@ -163,7 +182,9 @@
     up, down = (z + 1, col), (z - 1, col)
     ring = [lax.rem(z + k, rows) for k in range(rows)]
     side = 1 - 2 * (z // (rows // 2))
-    near = [z] + [lax.rem(z + side * k + rows, rows) for k in range(1, rows)]
+    steps = [lax.rem(z + side * k + rows, rows) for k in range(1, rows)]
+    outer = z // (rows - 1) + (rows - 1 - z) // (rows - 1)
+    near = [z, steps[0], outer * steps[1] + (1 - outer) * steps[2], outer * steps[2] + (1 - outer) * steps[1]]
 
     loads = []
     for k, (src, dst) in enumerate([(w1h, w1f), (w2h, w2f), (clean, cl), (noise, no)]):
@@ -177,12 +198,15 @@
     pending = []
 
     def sem(kind, at):
-        return sems.at[names.setdefault(kind, len(names)), at]
+        count = 1 if kind in SINGLE else rows
+        if kind not in names:
+            names[kind] = sum(size for _, size in names.values()), count
+        return sems.at[names[kind][0] + (0 if count == 1 else at)]
 
     def remote(src, dst, kind, at_send, at_recv, dev):
         return pltpu.make_async_remote_copy(
             src_ref=src, dst_ref=dst, send_sem=sem("s" + kind, at_send),
-            recv_sem=sem("r" + kind[:2], at_recv), device_id=dev, device_id_type=MESH,
+            recv_sem=sem("r" + kind.split("_")[-1], at_recv), device_id=dev, device_id_type=MESH,
         )
 
     def when(cond, fn):
@@ -193,7 +217,8 @@
 
     def send(cond, *spec):
         when(cond, lambda: remote(*spec).start())
-        pending.append((cond, spec))
+        if spec[2].startswith("z_") or "s" + spec[2] not in SINGLE:
+            pending.append((cond, spec))
 
     def arrive(cond, dst, kind, at):
         flag = sem("r" + kind, at)
@@ -204,15 +229,37 @@
     def span(start, size, unit):
         return pl.ds(pl.multiple_of(start, unit), size)
 
-    def cut(m):
-        return round_up(hp // 2, 16) if m == 0 else hp - round_up(hp // 2, 16)
-
     def part_rows(m, p):
-        return (0, cut(m)) if p == 0 else (cut(m), hp - cut(m))
+        size = hp if m == 0 else tp
+        cut = round_up(size // 2, 16) if m == 0 else size // 2 // 16 * 16
+        return (0, cut) if p == 0 else (cut, size - cut)
 
     def wblk(m, xyb, zb, p=None):
-        lo, size = (0, hp) if p is None else part_rows(m, p)
-        return w.at[m, span(xyb * hp + lo, size, 16), span(zb * ip, ip, 128)]
+        lo, size = (0, hp if m == 0 else tp) if p is None else part_rows(m, p)
+        if m == 1:
+            return wt.at[xyb, zb, slice(lo, lo + size), :]
+        return w.at[0, span(xyb * hp + lo, size, 16), span(zb * ip, ip, 128)]
+
+    tile_lane = lax.broadcasted_iota(jnp.int32, (hp, 128), 1)
+
+    def fold(tail):
+        turned = pltpu.roll(tail, 128 - carried, 1)
+        folded = jnp.zeros((group, 128), f32)
+        for q in range(128 // left):
+            piece = turned[q * group : min((q + 1) * group, hp), :]
+            piece = jnp.pad(piece, ((0, group - piece.shape[0]), (0, 0)))
+            piece = piece if q == 0 else pltpu.roll(piece, left * q, 1)
+            folded = jnp.where(tile_lane[:group] // left == q, piece, folded)
+        return turned, folded
+
+    def unfold(top, folded):
+        pieces = []
+        for q in range(128 // left):
+            piece = folded if q == 0 else pltpu.roll(folded, 128 - left * q, 1)
+            pieces.append(piece[: min(group, hp - q * group), :])
+        turned = jnp.where(tile_lane < left, jnp.concatenate(pieces, axis=0), top)
+        tail = pltpu.roll(turned, carried, 1)
+        return jnp.where(tile_lane < carried + left, tail, 0.0)
 
     def chan(zb, size=ib):
         return span(zb * ip, size, 16)
@@ -228,9 +275,10 @@
         tg[pad, :] = jnp.zeros((ip - ib, sub), bf16)
 
     line = lax.broadcasted_iota(jnp.int32, (hp, ip), 0)
-    for m, full in enumerate((w1f, w2f)):
+    blocks = []
+    for m, whole in enumerate((w1f, w2f)):
         loads[m].wait()
-        block = jnp.pad(full[...], ((0, hp - hb), (0, ip - ib)))
+        block = jnp.pad(whole[...], ((0, hp - hb), (0, ip - ib)))
         if m == 0:
             total = jnp.sum(block * block, axis=1, keepdims=True)
             total = jnp.pad(jnp.broadcast_to(total, (hp, 128)), ((0, 256 - hp), (0, 0)))
@@ -240,14 +288,33 @@
         high, low = split_sum(total)
         block = jnp.where(line == hb, high.astype(f32), block)
         block = jnp.where(line == hb + 1, low.astype(f32), block)
-        w[m, span(xy * hp, hp, 16), span(z * ip, ip, 128)] = block.astype(bf16)
+        blocks.append(block)
+    turned, folded = fold(blocks[1][:, full:])
+    first_tail = jnp.where(tile_lane < ib - full, blocks[0][:, full:], turned)
+    w[0, span(xy * hp, hp, 16), span(z * ip, full, 128)] = blocks[0][:, :full].astype(bf16)
+    w[0, span(xy * hp, hp, 16), span(z * ip + full, 128, 128)] = first_tail.astype(bf16)
+    for k in range(full // 128):
+        wt[xy, z, k * hp : (k + 1) * hp, :] = blocks[1][:, k * 128 : (k + 1) * 128].astype(bf16)
+    wt[xy, z, full // 128 * hp :, :] = folded.astype(bf16)
     pl.semaphore_wait(barrier, len(peers))
 
-    def along_z(cond, m, zb, go_up, go_down):
+    def along_z(cond, m, zb, go_up, go_down, p=None):
+        kind = f"z{m}{'' if p is None else p}"
+        block = wblk(m, xy, zb, p)
         if go_up:
-            send(both(cond, z + 1 < rows), wblk(m, xy, zb), wblk(m, xy, zb), f"z{m}u", zb, zb, up)
+            send(both(cond, z + 1 < rows), block, block, kind, z, zb, up)
         if go_down:
-            send(both(cond, z > 0), wblk(m, xy, zb), wblk(m, xy, zb), f"z{m}d", zb, zb, down)
+            send(both(cond, z > 0), block, block, "z_" + kind, 0, zb, down)
+
+    def gather_wait(kind, region):
+        flag = sem(kind, 0)
+        copies = pltpu.make_async_remote_copy(
+            src_ref=region, dst_ref=region, send_sem=flag, recv_sem=flag, device_id=dev_p, device_id_type=MESH,
+        )
+        if kind[0] == "s":
+            copies.wait_send()
+        else:
+            copies.wait_recv()
 
     def both(a, b):
         return b if a is None else jnp.logical_and(a, b)
@@ -265,10 +332,16 @@
     def sides(d):
         return ((z - d >= 0, z - d, True, False), (z + d < rows, z + d, False, True))
 
-    def hop(m, d):
-        for cond, zb, go_up, go_down in sides(d):
-            arrive(cond, wblk(m, xy, zb), f"z{m}", zb)
-            along_z(cond, m, zb, go_up and d < rows - 1, go_down and d < rows - 1)
+    def hop(m, d, p=None, signs=(-1, 1)):
+        kind = f"z{m}{'' if p is None else p}"
+        for sign in signs:
+            zb, zt = z + sign * side * d, z - sign * side
+            inside = jnp.logical_and(zb >= 0, zb < rows)
+            block = wblk(m, xy, zb, p)
+            arrive(inside, block, kind, zb)
+            if d < rows - 1:
+                onward = jnp.logical_and(inside, jnp.logical_and(zt >= 0, zt < rows))
+                send(onward, block, block, kind, zb, zb, (zt, col))
 
     def each_side(fn, m, d):
         if d == 0:
@@ -277,8 +350,11 @@
             for cond, zb, _, _ in sides(d):
                 fn(cond, m, zb)
 
-    for m in range(2):
-        along_z(None, m, z, True, True)
+    end = jnp.logical_or(z == 0, z == rows - 1)
+    middle = jnp.logical_not(end)
+    for p in range(2):
+        along_z(None, 0, z, True, True, p)
+    along_z(end, 1, z, True, True)
     for m in range(2):
         across(None, m, z)
 
@@ -298,34 +374,48 @@
     def state_to_partner(zb):
         send(None, st.at[chan(zb), mine], st.at[chan(zb), other], "f", zb, zb, dev_p)
 
-    hop(0, 1)
+    def toward(kind, first, d):
+        plane, target = (0, st.at[chan(z), mine]) if kind == "t" else (1, tg.at[chan(z), :])
+        for direction, steps in ((1, z), (-1, rows - 1 - z)):
+            zt = z + direction * d
+            send(steps == first, sto.at[plane, :, pix(zt)], target,
+                 kind, 0, z, (zt, col))
+
+    def some(fn, wanted, m, d):
+        for cond, zb, _, _ in sides(d):
+            fn(jnp.logical_and(cond, wanted), m, zb)
+
+    toward("t", 0, 1)
+    state_to_partner(z)
+    hop(0, 1, 0)
+    hop(0, 1, 1)
+    along_z(middle, 1, z, True, True)
     each_side(across, 0, 1)
     each_side(diagonal, 0, 0)
-    hop(1, 1)
-    for k in range(1, rows):
-        send(None, sto.at[0, :, pix(ring[k])], st.at[chan(z), mine], "t", k, z, (ring[k], col))
-    state_to_partner(z)
+    hop(1, 1, None, (-1,))
     each_side(diagonal, 1, 0)
-    if rows > 2:
-        hop(0, 2)
-        each_side(across, 0, 2)
+    hop(0, 2, 0)
+    hop(0, 2, 1)
+    each_side(across, 0, 2)
+    hop(1, 1, None, (1,))
+    toward("t", 1, 1)
+    toward("t", 2, 1)
+    each_side(diagonal, 0, 1)
+    hop(0, 3, 0)
+    hop(0, 3, 1)
+    each_side(across, 0, 3)
+    hop(1, 2)
+    toward("t", 0, 2)
+    toward("t", 1, 2)
+    each_side(diagonal, 0, 2)
     each_side(across, 1, 1)
-    each_side(diagonal, 0, 1)
-    if rows > 2:
-        hop(1, 2)
-    for k in range(1, rows):
-        zt = near[k]
-        send(None, sto.at[1, :, pix(zt)], tg.at[chan(z), :], "g", k, z, (zt, col))
-    for d in range(3, rows):
-        hop(0, d)
-        each_side(across, 0, d)
-    if rows > 2:
-        each_side(diagonal, 0, 2)
-    each_side(diagonal, 1, 1)
-    for d in range(3, rows):
-        hop(1, d)
-    for d in range(2, rows):
-        each_side(across, 1, d)
+    each_side(across, 1, 2)
+    toward("t", 0, 3)
+    each_side(diagonal, 0, 3)
+    hop(1, 3)
+    each_side(across, 1, 3)
+    toward("g", 1, 1)
+    toward("g", 0, 1)
     stack = []
     for j in range(CORES):
         whose = core if j == 0 else 1 - core
@@ -335,15 +425,15 @@
             pieces = [row[:, (b * CORES + c) * hb : (b * CORES + c + 1) * hb] for c in range(CORES)]
             piece = jnp.where(core == 0, pieces[0], pieces[1])
             stack.append(jnp.pad(piece, ((0, 0), (0, 256 - hb))))
-    for k in range(1, rows):
-        zb = ring[rows - k]
+    def take_state(k):
+        zb = near[k]
         arrive(None, st.at[chan(zb), mine], "t", zb)
         state_to_partner(zb)
-    for d in range(3, rows):
-        each_side(diagonal, 0, d)
-    for zb in range(rows):
-        arrive(None, wblk(0, dn, zb, 0), "a0", zb)
-        arrive(None, wblk(0, dn, zb, 1), "b0", zb)
+
+    take_state(1)
+    for p in range(2):
+        lo, size = part_rows(0, p)
+        gather_wait(f"r{'ab'[p]}0", w.at[0, span(dn * hp + lo, size, 16), :])
 
     def sums_of(m, b, lanes):
         tail = w[m, (b + 1) * hp - 16 : (b + 1) * hp, lanes].astype(f32)
@@ -361,30 +451,29 @@
             gain[j, at, :] = jnp.broadcast_to(columns[:hp, k : k + 1], (hp, 128))
         k = CORES * chips + b
         nrm[at, :] = jnp.broadcast_to(jnp.sqrt(1.0 + columns[:hp, k : k + 1]), (hp, 128))
-    for zb in range(rows):
+    half_rows = hh // 2
+
+    def forward(k):
+        zb = near[k]
         arrive(None, st.at[chan(zb), other], "f", zb)
-
-    half_rows = hh // 2
-
-    def forward(part):
-        at = slice(part * half_rows, (part + 1) * half_rows)
-        value = jnp.dot(w[0, at, :], st[...], preferred_element_type=f32)
-        inverse = twice(1.0 / nrm[at, :])
-        for j in range(CORES):
-            lanes = slice(j * sub, (j + 1) * sub)
-            v = value[:, lanes] * inverse
-            sig = jax.nn.sigmoid(v)
-            scale = twice(gain[j, at, :]) * SILU_GAIN
-            pre[at, lanes] = v
-            hid[at, lanes] = (v * sig * scale).astype(bf16)
-            slp[at, lanes] = sig * (1.0 + v * (1.0 - sig)) * scale
-
-    forward(0)
-    if rows > 2:
-        each_side(diagonal, 1, 2)
-    forward(1)
-    for d in range(3, rows):
-        each_side(diagonal, 1, d)
+        at_in = span(zb * ip, ip, 128)
+        for part in range(2):
+            at = slice(part * half_rows, (part + 1) * half_rows)
+            value = jnp.dot(w[0, at, at_in], st[at_in, :], preferred_element_type=f32)
+            if k > 0:
+                value = value + pre[at, :]
+            if k < rows - 1:
+                pre[at, :] = value
+                continue
+            inverse = twice(1.0 / nrm[at, :])
+            for j in range(CORES):
+                lanes = slice(j * sub, (j + 1) * sub)
+                v = value[:, lanes] * inverse
+                sig = jax.nn.sigmoid(v)
+                scale = twice(gain[j, at, :]) * SILU_GAIN
+                pre[at, lanes] = v
+                hid[at, lanes] = (v * sig * scale).astype(bf16)
+                slp[at, lanes] = sig * (1.0 + v * (1.0 - sig)) * scale
 
     def zlanes(zb):
         return span(zb * ip, ip, 128)
@@ -394,13 +483,20 @@
         at = zlanes(zb)
         arrive(None, wblk(1, dn, zb, 0), "a1", zb)
         arrive(None, wblk(1, dn, zb, 1), "b1", zb)
+        for b in range(chips):
+            rows_at = slice(b * hp, (b + 1) * hp)
+            for k in range(full // 128):
+                w[1, rows_at, span(zb * ip + k * 128, 128, 128)] = wt[b, zb, k * hp : (k + 1) * hp, :]
+            tail_at = span(zb * ip + full, 128, 128)
+            tail = unfold(w[0, rows_at, tail_at].astype(f32), wt[b, zb, full // 128 * hp :, :].astype(f32))
+            w[1, rows_at, tail_at] = tail.astype(bf16)
         total = sum(sums_of(1, b, at) for b in range(chips))
         s2[0, :, at] = jnp.broadcast_to(total, (s2.shape[1], ip))
         send(None, s2.at[0, :, at], s2.at[1, :, at], "n", i, zb, dev_p)
-        full = lax.dot_general(w[1, :, at], hid[...], CONTRACT_LEAD, preferred_element_type=f32)
-        brp[at, :] = full[:, other]
+        partial = lax.dot_general(w[1, :, at], hid[...], CONTRACT_LEAD, preferred_element_type=f32)
+        brp[at, :] = partial[:, other]
         send(None, brp.at[at, :], brr.at[at, :], "p", i, zb, dev_p)
-        brk[at, :] = full[:, mine]
+        brk[at, :] = partial[:, mine]
 
     def slope_part(i):
         zb = near[i]
@@ -434,11 +530,18 @@
         second = lax.dot_general(hid[...], dbr[at, :], CONTRACT_TAIL, preferred_element_type=f32)
         dot2 = d2[0, :1, at] + d2[1, :1, at]
         for b in range(chips):
-            part = second[b * hp : (b + 1) * hp, :]
-            g[1, b * hp : (b + 1) * hp, at] = jnp.where(hidden_line >= hb, dot2, part).astype(bf16)
+            rows_at = slice(b * hp, (b + 1) * hp)
+            part = jnp.where(hidden_line >= hb, dot2, second[rows_at, :])
+            for k in range(full // 128):
+                gt[b, i, k * hp : (k + 1) * hp, :] = part[:, k * 128 : (k + 1) * 128].astype(bf16)
+            turned, folded = fold(part[:, full:])
+            gt[b, i, full // 128 * hp :, :] = folded.astype(bf16)
+            g[rows_at, span(zb * ip + full, 128, 128)] = turned.astype(bf16)
         total = jnp.broadcast_to(1.0 + s2[0, :1, at] + s2[1, :1, at], (128, ip))
         inverse = 1.0 / jnp.sqrt(total.T)
         db2[at, other] = (dbr[at, other].astype(f32) * twice(inverse)).astype(bf16)
+
+    dot_rows = []
 
     def backward():
         for part in range(2):
@@ -448,73 +551,110 @@
             dpre[at, :] = rounded
             total = jnp.sum(rounded.astype(f32) * pre[at, :], axis=1, keepdims=True)
             dot1[at, :] = total * nrm[at, :]
+        for b in range(chips):
+            column = jnp.pad(dot1[b * hp : (b + 1) * hp, :], ((0, 256 - hp), (0, 0)))
+            dot_rows.append(jnp.pad(column.T[:1, :], ((0, 0), (0, ip - 256))))
 
     lane = lax.broadcasted_iota(jnp.int32, (1, ip), 1)
-    last = [ring[k] for k in range(1, rows)] + [z]
+    last = near[:0:-1] + [z]
     orders = (last, near)
 
     def first_part(i):
         zb = last[i]
         at = zlanes(zb)
         first = lax.dot_general(dpre[...], st[at, :], CONTRACT_TAIL, preferred_element_type=f32)
-        g[0, :, at] = jnp.where(lane >= ib, dot1[:, :1], first).astype(bf16)
-
-    def gblk(m, xyb, zb, p):
+        tail_at = span(zb * ip + full, 128, 128)
+        for b in range(chips):
+            rows_at = slice(b * hp, (b + 1) * hp)
+            part = jnp.where(hidden_line >= hb, dot_rows[b], first[rows_at, :])
+            g[rows_at, span(zb * ip, full, 128)] = part[:, :full].astype(bf16)
+            turned = g[rows_at, tail_at].astype(f32)
+            g[rows_at, tail_at] = jnp.where(tile_lane < ib - full, part[:, full:], turned).astype(bf16)
+
+    def gblk(m, xyb, i, p):
         lo, size = part_rows(m, p)
-        return (m, span(xyb * hp + lo, size, 16), span(zb * ip, ip, 128))
-
-    def rblk(ref, m, i, p):
+        if m == 1:
+            return gt, (xyb, i, slice(lo, lo + size), slice(None))
+        return g, (span(xyb * hp + lo, size, 16), span(last[i] * ip, ip, 128))
+
+    def gref(m, xyb, i, p):
+        ref, at = gblk(m, xyb, i, p)
+        return ref.at[at]
+
+    def gval(m, xyb, i, p):
+        ref, at = gblk(m, xyb, i, p)
+        return ref[at].astype(f32)
+
+    def rblk_all(refs, m, lo, size):
+        return refs[m].at[:, slice(lo, lo + size), :]
+
+    def rblk(refs, m, i, p):
         lo, size = part_rows(m, p)
-        return ref.at[m, i, slice(lo, lo + size), :]
+        return refs[m].at[i, slice(lo, lo + size), :]
 
     def legs(p):
         return (yn, dev_y, xn, dev_x) if p == 0 else (xn, dev_x, yn, dev_y)
 
     def stage_a(m, i):
-        zb = orders[m][i]
         for p in range(2):
             nb1, dev1, nb2, dev2 = legs(p)
-            send(None, g.at[gblk(m, dn, zb, p)], rblk(ra, m, i, p), f"{'AB'[p]}{m}", i, i, dev1)
+            send(None, gref(m, dn, i, p), rblk(ra, m, i, p), f"{'AB'[p]}{m}", i, i, dev1)
         for p in range(2):
             nb1, dev1, nb2, dev2 = legs(p)
-            send(None, g.at[gblk(m, nb1, zb, p)], rblk(rc, m, i, p), f"{'CD'[p]}{m}", i, i, dev1)
+            send(None, gref(m, nb1, i, p), rblk(rc, m, i, p), f"{'CD'[p]}{m}", i, i, dev1)
 
     def stage_b(m, i):
-        zb = orders[m][i]
         for p in range(2):
             nb1, dev1, nb2, dev2 = legs(p)
             arrive(None, rblk(ra, m, i, p), f"{'AB'[p]}{m}", i)
             lo, size = part_rows(m, p)
-            inside = (m, i, slice(lo, lo + size))
-            sa[inside] = (g[gblk(m, nb2, zb, p)].astype(f32) + ra[inside].astype(f32)).astype(bf16)
+            inside = (i, slice(lo, lo + size))
+            sa[m][inside] = (gval(m, nb2, i, p) + ra[m][inside].astype(f32)).astype(bf16)
             send(None, rblk(sa, m, i, p), rblk(rb, m, i, p), f"{'EF'[p]}{m}", i, i, dev2)
 
     def stage_c(m, i):
-        zb = orders[m][i]
+        totals = []
         for p in range(2):
             arrive(None, rblk(rc, m, i, p), f"{'CD'[p]}{m}", i)
             arrive(None, rblk(rb, m, i, p), f"{'EF'[p]}{m}", i)
-        own = g[m, span(xy * hp, hp, 16), span(zb * ip, ip, 128)].astype(f32)
-        total = own + rb[m, i].astype(f32) + rc[m, i].astype(f32)
+            lo, size = part_rows(m, p)
+            inside = (i, slice(lo, lo + size))
+            totals.append(gval(m, xy, i, p) + rb[m][inside].astype(f32) + rc[m][inside].astype(f32))
         own_at = rows - 1 if m == 0 else 0
+        total = jnp.concatenate(totals, axis=0)
         if i == own_at:
             return total
-        pz[m, i] = total.astype(bf16)
-        send(None, pz.at[m, i], rz.at[m, z], f"P{m}", i, z, (zb, col))
+        zb = orders[m][i]
+        pz[m][i] = total.astype(bf16)
+        send(None, pz[m].at[i], rz[m].at[z], f"P{m}", i, z, (zb, col))
         return None
 
     sums = [None, None]
+    forward(0)
+    forward(1)
+    some(diagonal, end, 1, 1)
+    take_state(2)
+    take_state(3)
+    toward("g", 2, 1)
+    forward(2)
+    forward(3)
+    toward("g", 0, 2)
+    toward("g", 1, 2)
+    some(diagonal, middle, 1, 1)
+    some(diagonal, end, 1, 2)
     branch_part(0)
+    some(diagonal, middle, 1, 2)
+    each_side(diagonal, 1, 3)
+    slope_part(0)
+    toward("g", 0, 3)
+    second_part(0)
+    stage_a(1, 0)
     branch_part(1)
-    slope_part(0)
     branch_part(2)
     slope_part(1)
-    second_part(0)
-    stage_a(1, 0)
     branch_part(3)
     second_part(1)
     stage_a(1, 1)
-    stage_b(1, 0)
     slope_part(2)
     second_part(2)
     stage_a(1, 2)
@@ -522,46 +662,79 @@
     slope_part(3)
     second_part(3)
     stage_a(1, 3)
-    sums[1] = stage_c(1, 0)
+    backward()
     stage_b(1, 2)
-    backward()
-    stage_b(1, 3)
     first_part(0)
     stage_a(0, 0)
+    first_part(1)
+    stage_b(1, 3)
+    stage_a(0, 1)
     stage_c(1, 1)
-    first_part(1)
-    stage_a(0, 1)
+    first_part(2)
+    stage_b(0, 0)
+    stage_a(0, 2)
     stage_c(1, 2)
-    stage_b(0, 0)
-    first_part(2)
-    stage_a(0, 2)
+    first_part(3)
+    stage_b(0, 1)
     stage_c(1, 3)
-    stage_b(0, 1)
-    first_part(3)
-    stage_a(0, 3)
     stage_c(0, 0)
     stage_b(0, 2)
+    stage_a(0, 3)
+    stage_b(1, 0)
     stage_c(0, 1)
+    stage_c(0, 2)
     stage_b(0, 3)
-    for k in range(1, rows):
-        arrive(None, rz.at[1, ring[k]], "P1", ring[k])
-    second = sums[1]
+    sums[1] = stage_c(1, 0)
+
+    def collect(m, total):
+        gather_wait(f"rP{m}", pz[m].at[0 : rows - 1])
+        for k in range(1, rows):
+            total = total + rz[m][ring[k]].astype(f32)
+        return total
+
+    second = collect(1, sums[1])
     norm2 = jnp.sqrt(1.0 + s2[0, :1, zlanes(z)] + s2[1, :1, zlanes(z)])[:, :ib]
-    for k in range(1, rows):
-        second = second + rz[1, ring[k]].astype(f32)
-    dot_second = second[hb : hb + 1, :ib]
-    out2[...] = second[:hb, :ib] / norm2 - w2f[...] * (dot_second / (norm2 * norm2 * norm2))
-    stage_c(0, 2)
-    first = stage_c(0, 3)
-    for k in range(1, rows):
-        arrive(None, rz.at[0, ring[k]], "P0", ring[k])
-        first = first + rz[0, ring[k]].astype(f32)
     norm1 = nrm[span(xy * hp, hp, 16), :1][:hb]
-    dot_first = first[:hb, ib : ib + 1]
-    out1[...] = first[:hb, :ib] / norm1 - w1f[...] * (dot_first / (norm1 * norm1 * norm1))
+    stores = [pltpu.make_async_copy(a, b, local_sems.at[4 + k])
+              for k, (a, b) in enumerate(((out1, out1h), (out2, out2h)))]
+    first = collect(0, stage_c(0, 3))
+
+    def finish():
+        row = jnp.broadcast_to(first[hb : hb + 1, :256], (128, 256))
+        dot_first = row.T[:hb, :1]
+        out1[...] = first[:hb, :ib] / norm1 - w1f[...] * (dot_first / (norm1 * norm1 * norm1))
+        stores[0].start()
+        tail = unfold(first[:, full:], second[full // 128 * hp :, :])
+        both_tiles = [second[k * hp : (k + 1) * hp, :] for k in range(full // 128)]
+        unpacked = jnp.concatenate(both_tiles + [tail], axis=1)
+        dot_second = unpacked[hb : hb + 1, :ib]
+        out2[...] = unpacked[:hb, :ib] / norm2 - w2f[...] * (dot_second / (norm2 * norm2 * norm2))
+        stores[1].start()
+
+    finish()
     for cond, spec in pending:
         when(cond, lambda spec=spec: remote(*spec).wait_send())
-    assert len(names) <= sems.shape[0], len(names)
+    for m in range(2):
+        for p in range(2):
+            lo, size = part_rows(m, p)
+            region = rblk_all(rb, m, lo, size)
+            for kind in ("ab"[p], "AB"[p], "CD"[p], "EF"[p]):
+                gather_wait(f"s{kind}{m}", region)
+        gather_wait(f"sP{m}", pz[m].at[0 : rows - 1])
+    for kind in ("x", "y"):
+        gather_wait(f"s{kind}0", w.at[0, :, 0:ip])
+        gather_wait(f"s{kind}1", wt.at[0])
+    gather_wait("sf", st.at[0 : rows * ib, mine])
+    gather_wait("st", st.at[0 : (rows - 1) * ib, mine])
+    gather_wait("sg", st.at[0 : (rows - 1) * ib, mine])
+    gather_wait("sp", brp)
+    gather_wait("sq", dbr.at[:, mine])
+    gather_wait("sn", s2.at[0])
+    gather_wait("sd", d2.at[0])
+    stores[0].wait()
+    stores[1].wait()
+    used = sum(size for _, size in names.values())
+    assert used == sems.shape[0], (used, sum(size == 1 for _, size in names.values()))
 
 
 def local_step(clean, noise, bucket, mod_table, w_first, w_second):
@@ -571,12 +744,14 @@
     own_rows = clean.shape[1]
     ib, hb = clean.shape[0], w_first.shape[2]
     sub = own_rows // rows
-    if sub != PIX or rows != 4:
+    full, carried, left, group = packing(hb, ib)
+    if sub != PIX or rows != 4 or left <= 0 or 128 % left != 0 or hb + 2 > 256:
         return local(clean, noise, bucket, mod_table, w_first, w_second)
     chips = cols // CORES
     hp, ip = round_up(hb + 2, 16), round_up(ib + 1, 128)
     bf16, f32 = jnp.bfloat16, jnp.float32
     hh, ii = chips * hp, rows * ip
+    tp = full // 128 * hp + group
     vmem = pl.BlockSpec(memory_space=pltpu.VMEM)
     smem = pl.BlockSpec(memory_space=pltpu.SMEM)
     anywhere = pl.BlockSpec(memory_space=pl.ANY)
@@ -584,7 +759,7 @@
         lambda *refs: step_kernel(hb, ib, samples, {}, *refs),
         out_shape=(jax.ShapeDtypeStruct((hb, ib), f32), jax.ShapeDtypeStruct((hb, ib), f32)),
         in_specs=[smem, anywhere, anywhere, vmem, anywhere, anywhere],
-        out_specs=(vmem, vmem),
+        out_specs=(anywhere, anywhere),
         scratch_shapes=[
             pltpu.VMEM((ib, own_rows), f32),
             pltpu.VMEM((ib, own_rows), f32),
@@ -592,6 +767,7 @@
             pltpu.VMEM((hb, ib), f32),
             pltpu.VMEM((2, ib, own_rows), bf16),
             pltpu.VMEM((2, hh, ii), bf16),
+            pltpu.VMEM((chips, rows, tp, 128), bf16),
             pltpu.VMEM((ii, CORES * sub), bf16),
             pltpu.VMEM((ii, sub), bf16),
             pltpu.VMEM((hh, 128), f32),
@@ -608,15 +784,24 @@
             pltpu.VMEM((2, 8, ii), f32),
             pltpu.VMEM((2, 8, ii), f32),
             pltpu.VMEM((hh, 128), f32),
-            pltpu.VMEM((2, hh, ii), bf16),
-            pltpu.VMEM((2, rows, hp, ip), bf16),
-            pltpu.VMEM((2, rows, hp, ip), bf16),
-            pltpu.VMEM((2, rows, hp, ip), bf16),
-            pltpu.VMEM((2, rows, hp, ip), bf16),
-            pltpu.VMEM((2, rows, hp, ip), bf16),
-            pltpu.VMEM((2, rows, hp, ip), bf16),
-            pltpu.SemaphoreType.DMA((80, rows)),
-            pltpu.SemaphoreType.DMA((4,)),
+            pltpu.VMEM((hh, ii), bf16),
+            pltpu.VMEM((chips, rows, tp, 128), bf16),
+            pltpu.VMEM((rows, hp, ip), bf16),
+            pltpu.VMEM((rows, tp, 128), bf16),
+            pltpu.VMEM((rows, hp, ip), bf16),
+            pltpu.VMEM((rows, tp, 128), bf16),
+            pltpu.VMEM((rows, hp, ip), bf16),
+            pltpu.VMEM((rows, tp, 128), bf16),
+            pltpu.VMEM((rows, hp, ip), bf16),
+            pltpu.VMEM((rows, tp, 128), bf16),
+            pltpu.VMEM((rows, hp, ip), bf16),
+            pltpu.VMEM((rows, tp, 128), bf16),
+            pltpu.VMEM((rows, hp, ip), bf16),
+            pltpu.VMEM((rows, tp, 128), bf16),
+            pltpu.VMEM((hb, ib), f32),
+            pltpu.VMEM((hb, ib), f32),
+            pltpu.SemaphoreType.DMA((31 * rows + 36,)),
+            pltpu.SemaphoreType.DMA((6,)),
         ],
         compiler_params=pltpu.CompilerParams(
             collective_id=0, has_side_effects=True, vmem_limit_bytes=60 * 1024 * 1024

time: 103 us -> 85.4 us (0.83)
  Pallas kernels: 99 us -> 81.1 us
    pallas_call x1, Pallas kernels: 99 us -> 81.1 us  [local_step(): pl.pallas_call(lambda *refs: step_kernel(hb, ib, samples, {}, *refs), out...]
where the time goes in v2:
time: 85.4 us; the launch traced here: 85.1 us
  Pallas kernels  81.1 us (95%)
  local copies, waits for them, and re-layouts  3.32 us (4%)
    pallas_call x1, Pallas kernels, local_step(): pl.pallas_call(lambda *refs: step_kernel(hb, ib, samples, {}, *refs), out...  81.1 us
    unnamed x2, local copies, waits for them, and re-layouts  3.32 us

profile of v2, /device:TPU:0, one launch (start us, length us, event | category | flops | bytes accessed | tf_op | source)
XLA Modules:
  0.0 85.1 jit_solution(12919612992168580517)
XLA Ops:
  0.6 81.1 %shard_map.77 = (f32[168,336]{1,0:T(8,128)}, f32[168,336]{1,0:T(8,128)}) custom-call(s32[32]{0:T(128)} %refs_0_.1, f32[336,1024]{1,0:T(8,128)} %refs_1_.1, f32[336,1024]{1,0:T(8,128)} %refs_2_.1, f32[32,1344]{1,0:T(8,128)} %bitcast.13, f32[168,336]{1,0:T(8,128)} %bitcast.9, f32[168,336]{1,0:T(8,128)} %bitcast.10), custom_call_target="tpu_custom_call" | custom-call | tf_op jit(solution)/shard_map/pallas_call | solution.py:758
  81.8 1.7 %copy.10 = f32[1,336,168]{1,2,0:T(8,128)} copy(f32[1,336,168]{1,2,0:T(8,128)} %bitcast.12) | data formatting | bytes 451584
  83.4 1.7 %copy.11 = f32[1,168,336]{2,1,0:T(8,128)} copy(f32[1,168,336]{2,1,0:T(8,128)} %bitcast.11) | data formatting | bytes 451584

commit v3 on v2

--- a/solution.py
+++ b/solution.py
@@ -153,10 +153,10 @@
 
 
 def step_kernel(
-    hb, ib, samples, names, bucket, clean, noise, table, w1h, w2h, out1h, out2h,
+    hb, ib, samples, names, bucket_h, clean, noise, table_h, w1h, w2h, out1h, out2h,
     cl, no, w1f, w2f, sto, w, wt, st, tg, nrm, gain, pre, slp, hid, brk, brp, brr, dbr, db2, dpre,
     s2, d2, dot1, g, gt, ra0, ra1, sa0, sa1, rb0, rb1, rc0, rc1, pz0, pz1, rz0, rz1, out1, out2,
-    sems, local_sems,
+    bucket, table, sems, local_sems,
 ):
     ra, sa, rb, rc, pz, rz = (ra0, ra1), (sa0, sa1), (rb0, rb1), (rc0, rc1), (pz0, pz1), (rz0, rz1)
     rows = st.shape[0] // round_up(ib + 1, 128)
@@ -184,10 +184,12 @@
     side = 1 - 2 * (z // (rows // 2))
     steps = [lax.rem(z + side * k + rows, rows) for k in range(1, rows)]
     outer = z // (rows - 1) + (rows - 1 - z) // (rows - 1)
-    near = [z, steps[0], outer * steps[1] + (1 - outer) * steps[2], outer * steps[2] + (1 - outer) * steps[1]]
+    near = [z] + [outer * steps[k] + (1 - outer) * steps[(k + 2) % 3] for k in range(3)]
 
     loads = []
-    for k, (src, dst) in enumerate([(w1h, w1f), (w2h, w2f), (clean, cl), (noise, no)]):
+    for k, (src, dst) in enumerate([
+        (w1h, w1f), (w2h, w2f), (clean, cl), (noise, no), (bucket_h, bucket), (table_h, table)
+    ]):
         loads.append(pltpu.make_async_copy(src, dst, local_sems.at[k]))
         loads[-1].start()
     barrier = pltpu.get_barrier_semaphore()
@@ -330,13 +332,18 @@
         send(cond, wblk(m, yn, zb, 1), wblk(m, yn, zb, 1), f"b{m}", zb, zb, dev_x)
 
     def sides(d):
-        return ((z - d >= 0, z - d, True, False), (z + d < rows, z + d, False, True))
-
-    def hop(m, d, p=None, signs=(-1, 1)):
+        found = []
+        for sign in (-1, 1):
+            zb = z + sign * side * d
+            found.append((jnp.logical_and(zb >= 0, zb < rows), zb))
+        return found
+
+    def hop(m, d, p=None, signs=(-1, 1), who=None):
         kind = f"z{m}{'' if p is None else p}"
         for sign in signs:
             zb, zt = z + sign * side * d, z - sign * side
             inside = jnp.logical_and(zb >= 0, zb < rows)
+            inside = inside if who is None else jnp.logical_and(inside, who)
             block = wblk(m, xy, zb, p)
             arrive(inside, block, kind, zb)
             if d < rows - 1:
@@ -347,7 +354,7 @@
         if d == 0:
             fn(None, m, z)
         else:
-            for cond, zb, _, _ in sides(d):
+            for cond, zb in sides(d):
                 fn(cond, m, zb)
 
     end = jnp.logical_or(z == 0, z == rows - 1)
@@ -360,6 +367,8 @@
 
     loads[2].wait()
     loads[3].wait()
+    loads[4].wait()
+    loads[5].wait()
     for k in range(rows):
         lanes = slice(k * sub, (k + 1) * sub)
         picked = jnp.full((1, sub), bucket[col * rows + k], jnp.int32)
@@ -382,7 +391,7 @@
                  kind, 0, z, (zt, col))
 
     def some(fn, wanted, m, d):
-        for cond, zb, _, _ in sides(d):
+        for cond, zb in sides(d):
             fn(jnp.logical_and(cond, wanted), m, zb)
 
     toward("t", 0, 1)
@@ -393,7 +402,6 @@
     each_side(across, 0, 1)
     each_side(diagonal, 0, 0)
     hop(1, 1, None, (-1,))
-    each_side(diagonal, 1, 0)
     hop(0, 2, 0)
     hop(0, 2, 1)
     each_side(across, 0, 2)
@@ -401,19 +409,20 @@
     toward("t", 1, 1)
     toward("t", 2, 1)
     each_side(diagonal, 0, 1)
+    each_side(diagonal, 1, 0)
     hop(0, 3, 0)
     hop(0, 3, 1)
     each_side(across, 0, 3)
-    hop(1, 2)
     toward("t", 0, 2)
+    hop(1, 2, None, (-1, 1), middle)
     toward("t", 1, 2)
     each_side(diagonal, 0, 2)
     each_side(across, 1, 1)
-    each_side(across, 1, 2)
+    some(across, middle, 1, 2)
+    each_side(diagonal, 0, 3)
     toward("t", 0, 3)
-    each_side(diagonal, 0, 3)
-    hop(1, 3)
-    each_side(across, 1, 3)
+    hop(1, 2, None, (-1, 1), end)
+    some(across, end, 1, 2)
     toward("g", 1, 1)
     toward("g", 0, 1)
     stack = []
@@ -478,7 +487,7 @@
     def zlanes(zb):
         return span(zb * ip, ip, 128)
 
-    def branch_part(i):
+    def open_second(i):
         zb = near[i]
         at = zlanes(zb)
         arrive(None, wblk(1, dn, zb, 0), "a1", zb)
@@ -493,6 +502,10 @@
         total = sum(sums_of(1, b, at) for b in range(chips))
         s2[0, :, at] = jnp.broadcast_to(total, (s2.shape[1], ip))
         send(None, s2.at[0, :, at], s2.at[1, :, at], "n", i, zb, dev_p)
+
+    def branch_part(i):
+        zb = near[i]
+        at = zlanes(zb)
         partial = lax.dot_general(w[1, :, at], hid[...], CONTRACT_LEAD, preferred_element_type=f32)
         brp[at, :] = partial[:, other]
         send(None, brp.at[at, :], brr.at[at, :], "p", i, zb, dev_p)
@@ -525,9 +538,16 @@
     def second_part(i):
         zb = near[i]
         at = zlanes(zb)
+        if i == 0:
+            second = lax.dot_general(hid[:, mine], dbr[at, mine], CONTRACT_TAIL, preferred_element_type=f32)
         arrive(None, dbr.at[at, other], "q", zb)
         arrive(None, d2.at[1, :, at], "d", zb)
-        second = lax.dot_general(hid[...], dbr[at, :], CONTRACT_TAIL, preferred_element_type=f32)
+        if i == 0:
+            second = second + lax.dot_general(
+                hid[:, other], dbr[at, other], CONTRACT_TAIL, preferred_element_type=f32
+            )
+        else:
+            second = lax.dot_general(hid[...], dbr[at, :], CONTRACT_TAIL, preferred_element_type=f32)
         dot2 = d2[0, :1, at] + d2[1, :1, at]
         for b in range(chips):
             rows_at = slice(b * hp, (b + 1) * hp)
@@ -632,10 +652,13 @@
     sums = [None, None]
     forward(0)
     forward(1)
+    hop(1, 3)
+    each_side(across, 1, 3)
     some(diagonal, end, 1, 1)
     take_state(2)
     take_state(3)
     toward("g", 2, 1)
+    open_second(0)
     forward(2)
     forward(3)
     toward("g", 0, 2)
@@ -645,16 +668,20 @@
     branch_part(0)
     some(diagonal, middle, 1, 2)
     each_side(diagonal, 1, 3)
+    open_second(1)
+    branch_part(1)
     slope_part(0)
     toward("g", 0, 3)
+    slope_part(1)
     second_part(0)
     stage_a(1, 0)
-    branch_part(1)
+    open_second(2)
     branch_part(2)
-    slope_part(1)
-    branch_part(3)
     second_part(1)
     stage_a(1, 1)
+    open_second(3)
+    branch_part(3)
+    stage_b(1, 0)
     slope_part(2)
     second_part(2)
     stage_a(1, 2)
@@ -680,7 +707,6 @@
     stage_c(0, 0)
     stage_b(0, 2)
     stage_a(0, 3)
-    stage_b(1, 0)
     stage_c(0, 1)
     stage_c(0, 2)
     stage_b(0, 3)
@@ -695,7 +721,7 @@
     second = collect(1, sums[1])
     norm2 = jnp.sqrt(1.0 + s2[0, :1, zlanes(z)] + s2[1, :1, zlanes(z)])[:, :ib]
     norm1 = nrm[span(xy * hp, hp, 16), :1][:hb]
-    stores = [pltpu.make_async_copy(a, b, local_sems.at[4 + k])
+    stores = [pltpu.make_async_copy(a, b, local_sems.at[6 + k])
               for k, (a, b) in enumerate(((out1, out1h), (out2, out2h)))]
     first = collect(0, stage_c(0, 3))
 
@@ -737,6 +763,11 @@
     assert used == sems.shape[0], (used, sum(size == 1 for _, size in names.values()))
 
 
+def hand_over(in1, in2, out1, out2):
+    out1[...] = in1[...]
+    out2[...] = in2[...]
+
+
 def local_step(clean, noise, bucket, mod_table, w_first, w_second):
     rows = lax.axis_size("row")
     cols = lax.axis_size("col")
@@ -753,12 +784,11 @@
     hh, ii = chips * hp, rows * ip
     tp = full // 128 * hp + group
     vmem = pl.BlockSpec(memory_space=pltpu.VMEM)
-    smem = pl.BlockSpec(memory_space=pltpu.SMEM)
     anywhere = pl.BlockSpec(memory_space=pl.ANY)
     out1, out2 = pl.pallas_call(
         lambda *refs: step_kernel(hb, ib, samples, {}, *refs),
         out_shape=(jax.ShapeDtypeStruct((hb, ib), f32), jax.ShapeDtypeStruct((hb, ib), f32)),
-        in_specs=[smem, anywhere, anywhere, vmem, anywhere, anywhere],
+        in_specs=[anywhere] * 6,
         out_specs=(anywhere, anywhere),
         scratch_shapes=[
             pltpu.VMEM((ib, own_rows), f32),
@@ -800,13 +830,21 @@
             pltpu.VMEM((rows, tp, 128), bf16),
             pltpu.VMEM((hb, ib), f32),
             pltpu.VMEM((hb, ib), f32),
+            pltpu.SMEM(bucket.shape, jnp.int32),
+            pltpu.VMEM(mod_table.shape[1:], f32),
             pltpu.SemaphoreType.DMA((31 * rows + 36,)),
-            pltpu.SemaphoreType.DMA((6,)),
+            pltpu.SemaphoreType.DMA((8,)),
         ],
         compiler_params=pltpu.CompilerParams(
             collective_id=0, has_side_effects=True, vmem_limit_bytes=60 * 1024 * 1024
         ),
     )(bucket, clean, noise, mod_table[0], w_first[0].T, w_second[0])
+    out1, out2 = pl.pallas_call(
+        hand_over,
+        out_shape=(jax.ShapeDtypeStruct((hb, ib), f32), jax.ShapeDtypeStruct((hb, ib), f32)),
+        in_specs=[vmem] * 2,
+        out_specs=(vmem, vmem),
+    )(out1, out2)
     return (out1.T[None], out2[None])
 
 

time: 85.4 us -> 82.8 us (0.970)
  local copies, waits for them, and re-layouts: 3.32 us -> 0 us
  Pallas kernels: 81.1 us -> 82 us
    unnamed x2 -> x0, local copies, waits for them, and re-layouts: 3.32 us -> none
    pallas_call x0 -> x1, Pallas kernels: none -> 1.87 us  [local_step(): pl.pallas_call(hand_over, out_shape=(jax.ShapeDtypeStruct((hb, ib), f32),...]
    pallas_call x1, Pallas kernels: 81.1 us -> 80.1 us  [local_step(): pl.pallas_call(lambda *refs: step_kernel(hb, ib, samples, {}, *refs), out...]
where the time goes in v3:
time: 82.8 us; the launch traced here: 82.7 us
  Pallas kernels  82 us (99%)
    pallas_call x1, Pallas kernels, local_step(): pl.pallas_call(lambda *refs: step_kernel(hb, ib, samples, {}, *refs), out...  80.1 us
    pallas_call x1, Pallas kernels, local_step(): pl.pallas_call(hand_over, out_shape=(jax.ShapeDtypeStruct((hb, ib), f32),...  1.87 us

profile of v3, /device:TPU:0, one launch (start us, length us, event | category | flops | bytes accessed | tf_op | source)
XLA Modules:
  0.0 82.7 jit_solution(8928314730799015728)
XLA Ops:
  0.6 80.1 %shard_map.77 = (f32[168,336]{1,0:T(8,128)}, f32[168,336]{1,0:T(8,128)}) custom-call(s32[32]{0:T(128)} %refs_0_.1, f32[336,1024]{1,0:T(8,128)} %refs_1_.1, f32[336,1024]{1,0:T(8,128)} %refs_2_.1, f32[32,1344]{1,0:T(8,128)} %bitcast.11, f32[168,336]{1,0:T(8,128)} %bitcast.9, f32[168,336]{1,0:T(8,128)} %bitcast.10), custom_call_target="tpu_custom_call" | custom-call | tf_op jit(solution)/shard_map/pallas_call | solution.py:788
  80.8 1.9 %shard_map.78 = (f32[168,336]{1,0:T(8,128)}, f32[168,336]{1,0:T(8,128)}) custom-call(f32[168,336]{1,0:T(8,128)} %get-tuple-element.6.in1, f32[168,336]{1,0:T(8,128)} %get-tuple-element.7.in2), custom_call_target="tpu_custom_call" | custom-call | tf_op jit(solution)/shard_map/pallas_call | solution.py:842

commit v4 on v3

--- a/solution.py
+++ b/solution.py
@@ -633,20 +633,22 @@
             send(None, rblk(sa, m, i, p), rblk(rb, m, i, p), f"{'EF'[p]}{m}", i, i, dev2)
 
     def stage_c(m, i):
+        zb = orders[m][i]
+        own = i == (rows - 1 if m == 0 else 0)
         totals = []
         for p in range(2):
             arrive(None, rblk(rc, m, i, p), f"{'CD'[p]}{m}", i)
             arrive(None, rblk(rb, m, i, p), f"{'EF'[p]}{m}", i)
             lo, size = part_rows(m, p)
             inside = (i, slice(lo, lo + size))
-            totals.append(gval(m, xy, i, p) + rb[m][inside].astype(f32) + rc[m][inside].astype(f32))
-        own_at = rows - 1 if m == 0 else 0
-        total = jnp.concatenate(totals, axis=0)
-        if i == own_at:
-            return total
-        zb = orders[m][i]
-        pz[m][i] = total.astype(bf16)
-        send(None, pz[m].at[i], rz[m].at[z], f"P{m}", i, z, (zb, col))
+            total = gval(m, xy, i, p) + rb[m][inside].astype(f32) + rc[m][inside].astype(f32)
+            if own:
+                totals.append(total)
+            else:
+                pz[m][inside] = total.astype(bf16)
+                send(None, rblk(pz, m, i, p), rz[m].at[z, slice(lo, lo + size), :], f"P{m}", i, z, (zb, col))
+        if own:
+            return jnp.concatenate(totals, axis=0)
         return None
 
     sums = [None, None]
@@ -661,11 +663,11 @@
     open_second(0)
     forward(2)
     forward(3)
-    toward("g", 0, 2)
     toward("g", 1, 2)
     some(diagonal, middle, 1, 1)
     some(diagonal, end, 1, 2)
     branch_part(0)
+    toward("g", 0, 2)
     some(diagonal, middle, 1, 2)
     each_side(diagonal, 1, 3)
     open_second(1)
@@ -721,21 +723,17 @@
     second = collect(1, sums[1])
     norm2 = jnp.sqrt(1.0 + s2[0, :1, zlanes(z)] + s2[1, :1, zlanes(z)])[:, :ib]
     norm1 = nrm[span(xy * hp, hp, 16), :1][:hb]
-    stores = [pltpu.make_async_copy(a, b, local_sems.at[6 + k])
-              for k, (a, b) in enumerate(((out1, out1h), (out2, out2h)))]
     first = collect(0, stage_c(0, 3))
 
     def finish():
         row = jnp.broadcast_to(first[hb : hb + 1, :256], (128, 256))
         dot_first = row.T[:hb, :1]
-        out1[...] = first[:hb, :ib] / norm1 - w1f[...] * (dot_first / (norm1 * norm1 * norm1))
-        stores[0].start()
+        out1h[...] = first[:hb, :ib] / norm1 - w1f[...] * (dot_first / (norm1 * norm1 * norm1))
         tail = unfold(first[:, full:], second[full // 128 * hp :, :])
         both_tiles = [second[k * hp : (k + 1) * hp, :] for k in range(full // 128)]
         unpacked = jnp.concatenate(both_tiles + [tail], axis=1)
         dot_second = unpacked[hb : hb + 1, :ib]
-        out2[...] = unpacked[:hb, :ib] / norm2 - w2f[...] * (dot_second / (norm2 * norm2 * norm2))
-        stores[1].start()
+        out2h[...] = unpacked[:hb, :ib] / norm2 - w2f[...] * (dot_second / (norm2 * norm2 * norm2))
 
     finish()
     for cond, spec in pending:
@@ -757,8 +755,6 @@
     gather_wait("sq", dbr.at[:, mine])
     gather_wait("sn", s2.at[0])
     gather_wait("sd", d2.at[0])
-    stores[0].wait()
-    stores[1].wait()
     used = sum(size for _, size in names.values())
     assert used == sems.shape[0], (used, sum(size == 1 for _, size in names.values()))
 
@@ -787,9 +783,9 @@
     anywhere = pl.BlockSpec(memory_space=pl.ANY)
     out1, out2 = pl.pallas_call(
         lambda *refs: step_kernel(hb, ib, samples, {}, *refs),
-        out_shape=(jax.ShapeDtypeStruct((hb, ib), f32), jax.ShapeDtypeStruct((hb, ib), f32)),
+        out_shape=(pltpu.VMEM((hb, ib), f32), pltpu.VMEM((hb, ib), f32)),
         in_specs=[anywhere] * 6,
-        out_specs=(anywhere, anywhere),
+        out_specs=(vmem, vmem),
         scratch_shapes=[
             pltpu.VMEM((ib, own_rows), f32),
             pltpu.VMEM((ib, own_rows), f32),
@@ -844,7 +840,7 @@
         out_shape=(jax.ShapeDtypeStruct((hb, ib), f32), jax.ShapeDtypeStruct((hb, ib), f32)),
         in_specs=[vmem] * 2,
         out_specs=(vmem, vmem),
-    )(out1, out2)
+    )(*(pltpu.with_memory_space_constraint(out, pltpu.VMEM) for out in (out1, out2)))
     return (out1.T[None], out2[None])
 
 

time: 82.8 us -> 80.6 us (0.973)
  Pallas kernels: 82 us -> 79.3 us
    pallas_call x1, Pallas kernels: 80.1 us -> 78.4 us  [local_step(): pl.pallas_call(lambda *refs: step_kernel(hb, ib, samples, {}, *refs), out...]
    pallas_call x1, Pallas kernels: 1.87 us -> 0.82 us  [local_step(): pl.pallas_call(hand_over, out_shape=(jax.ShapeDtypeStruct((hb, ib), f32),...]
where the time goes in v4:
time: 80.6 us; the launch traced here: 79.9 us
  Pallas kernels  79.3 us (98%)
    pallas_call x1, Pallas kernels, local_step(): pl.pallas_call(lambda *refs: step_kernel(hb, ib, samples, {}, *refs), out...  78.4 us

profile of v4, /device:TPU:0, one launch (start us, length us, event | category | flops | bytes accessed | tf_op | source)
XLA Modules:
  0.0 79.9 jit_solution(9745840491287124553)
XLA Ops:
  0.6 78.4 %shard_map.77 = (f32[168,336]{1,0:T(8,128)S(1)}, f32[168,336]{1,0:T(8,128)S(1)}) custom-call(s32[32]{0:T(128)} %refs_0_.1, f32[336,1024]{1,0:T(8,128)} %refs_1_.1, f32[336,1024]{1,0:T(8,128)} %refs_2_.1, f32[32,1344]{1,0:T(8,128)} %bitcast.11, f32[168,336]{1,0:T(8,128)} %bitcast.9, f32[168,336]{1,0:T(8,128)} %bitcast.10), custom_call_target="tpu_custom_call" | custom-call | tf_op jit(solution)/shard_map/pallas_call | solution.py:784
  79.1 0.8 %shard_map.78 = (f32[168,336]{1,0:T(8,128)}, f32[168,336]{1,0:T(8,128)}) custom-call(f32[168,336]{1,0:T(8,128)S(1)} %get-tuple-element.6.in1, f32[168,336]{1,0:T(8,128)S(1)} %get-tuple-element.7.in2), custom_call_target="tpu_custom_call" | custom-call | tf_op jit(solution)/shard_map/pallas_call | solution.py:838

commit v5 on v4

--- a/solution.py
+++ b/solution.py
@@ -140,7 +140,7 @@
 
 
 SINGLE = set(
-    [f"s{kind}{m}" for kind in "abABCDEFPxy" for m in range(2)]
+    [f"s{kind}{m}" for kind in [*"abABCDPxy", "E_C", "F_D"] for m in range(2)]
     + ["s" + kind for kind in "ftgpqnd"] + ["ra0", "rb0", "rP0", "rP1"]
     + ["sz_z00", "sz_z01", "sz_z1"]
 )
@@ -615,13 +615,19 @@
     def legs(p):
         return (yn, dev_y, xn, dev_x) if p == 0 else (xn, dev_x, yn, dev_y)
 
-    def stage_a(m, i):
+    def far_leg(m, i):
         for p in range(2):
             nb1, dev1, nb2, dev2 = legs(p)
             send(None, gref(m, dn, i, p), rblk(ra, m, i, p), f"{'AB'[p]}{m}", i, i, dev1)
+
+    def near_leg(m, i):
         for p in range(2):
             nb1, dev1, nb2, dev2 = legs(p)
             send(None, gref(m, nb1, i, p), rblk(rc, m, i, p), f"{'CD'[p]}{m}", i, i, dev1)
+
+    def stage_a(m, i):
+        far_leg(m, i)
+        near_leg(m, i)
 
     def stage_b(m, i):
         for p in range(2):
@@ -630,16 +636,15 @@
             lo, size = part_rows(m, p)
             inside = (i, slice(lo, lo + size))
             sa[m][inside] = (gval(m, nb2, i, p) + ra[m][inside].astype(f32)).astype(bf16)
-            send(None, rblk(sa, m, i, p), rblk(rb, m, i, p), f"{'EF'[p]}{m}", i, i, dev2)
+            send(None, rblk(sa, m, i, p), rblk(rb, m, i, p), f"{'EF'[p]}_{'CD'[p]}{m}", i, i, dev2)
 
     def stage_c(m, i):
         zb = orders[m][i]
         own = i == (rows - 1 if m == 0 else 0)
         totals = []
         for p in range(2):
-            arrive(None, rblk(rc, m, i, p), f"{'CD'[p]}{m}", i)
-            arrive(None, rblk(rb, m, i, p), f"{'EF'[p]}{m}", i)
             lo, size = part_rows(m, p)
+            arrive(None, rb[m].at[0:2, slice(lo, lo + size), :], f"{'CD'[p]}{m}", i)
             inside = (i, slice(lo, lo + size))
             total = gval(m, xy, i, p) + rb[m][inside].astype(f32) + rc[m][inside].astype(f32)
             if own:
@@ -707,8 +712,9 @@
     stage_b(0, 1)
     stage_c(1, 3)
     stage_c(0, 0)
+    far_leg(0, 3)
     stage_b(0, 2)
-    stage_a(0, 3)
+    near_leg(0, 3)
     stage_c(0, 1)
     stage_c(0, 2)
     stage_b(0, 3)
@@ -742,7 +748,7 @@
         for p in range(2):
             lo, size = part_rows(m, p)
             region = rblk_all(rb, m, lo, size)
-            for kind in ("ab"[p], "AB"[p], "CD"[p], "EF"[p]):
+            for kind in ("ab"[p], "AB"[p], "CD"[p], "EF"[p] + "_" + "CD"[p]):
                 gather_wait(f"s{kind}{m}", region)
         gather_wait(f"sP{m}", pz[m].at[0 : rows - 1])
     for kind in ("x", "y"):
@@ -828,7 +834,7 @@
             pltpu.VMEM((hb, ib), f32),
             pltpu.SMEM(bucket.shape, jnp.int32),
             pltpu.VMEM(mod_table.shape[1:], f32),
-            pltpu.SemaphoreType.DMA((31 * rows + 36,)),
+            pltpu.SemaphoreType.DMA((27 * rows + 36,)),
             pltpu.SemaphoreType.DMA((8,)),
         ],
         compiler_params=pltpu.CompilerParams(

time: 80.6 us -> 80.4 us (level)
  no operation moved by 1% of the time
where the time goes in v5:
time: 80.4 us; the launch traced here: 79.8 us
  Pallas kernels  79.2 us (99%)
    pallas_call x1, Pallas kernels, local_step(): pl.pallas_call(lambda *refs: step_kernel(hb, ib, samples, {}, *refs), out...  78.4 us

profile of v5, /device:TPU:0, one launch (start us, length us, event | category | flops | bytes accessed | tf_op | source)
XLA Modules:
  0.0 79.8 jit_solution(5818599781594281443)
XLA Ops:
  0.6 78.4 %shard_map.77 = (f32[168,336]{1,0:T(8,128)S(1)}, f32[168,336]{1,0:T(8,128)S(1)}) custom-call(s32[32]{0:T(128)} %refs_0_.1, f32[336,1024]{1,0:T(8,128)} %refs_1_.1, f32[336,1024]{1,0:T(8,128)} %refs_2_.1, f32[32,1344]{1,0:T(8,128)} %bitcast.11, f32[168,336]{1,0:T(8,128)} %bitcast.9, f32[168,336]{1,0:T(8,128)} %bitcast.10), custom_call_target="tpu_custom_call" | custom-call | tf_op jit(solution)/shard_map/pallas_call | solution.py:790
  79.0 0.8 %shard_map.78 = (f32[168,336]{1,0:T(8,128)}, f32[168,336]{1,0:T(8,128)}) custom-call(f32[168,336]{1,0:T(8,128)S(1)} %get-tuple-element.6.in1, f32[168,336]{1,0:T(8,128)S(1)} %get-tuple-element.7.in2), custom_call_target="tpu_custom_call" | custom-call | tf_op jit(solution)/shard_map/pallas_call | solution.py:844
